TPU v7x, 32 devices: a whole 2x2x4 slice. The times are simulated.
32 devices in a mesh: batch: 4 (over x, core), rows: 8 (over z, y).
Axes of the slice: x: 2, y: 2, z: 4, core: 2. Of those that a mesh axis runs over, the one named last changes fastest.
Arguments:
- feat_quarter: bfloat16 [4, 128, 512, 256], P('batch', 'rows'), may hold values from -12 to 12
- feat_eighth: bfloat16 [4, 64, 256, 256], P('batch', 'rows'), may hold values from -12 to 12
- feat_sixteenth: bfloat16 [4, 32, 128, 256], P('batch', 'rows'), may hold values from -12 to 12
- feat_thirty: bfloat16 [4, 16, 64, 256], P('batch', 'rows'), may hold values from -12 to 12
- labels: int32 [4, 128, 512], P('batch', 'rows'), may hold values from 0 to 255, as said below
- first_weights: bfloat16 [4, 3, 3, 256, 128], replicated, may hold values from -0.125 to 0.125
- inner_weights: bfloat16 [3, 3, 3, 128, 128], replicated, may hold values from -0.1875 to 0.1875
- norm_gain: float32 [7, 128], replicated, may hold values from 0.1 to 1.9
- norm_shift: float32 [7, 128], replicated, may hold values from -3 to 3
- class_weight: bfloat16 [128, 19], replicated, may hold values from -0.5 to 0.5
- class_bias: float32 [19], replicated, may hold values from -3 to 3
Outputs:
- logits: bfloat16 [4, 19, 128, 512], P('batch', None, 'rows')
- mean_loss: float32 [], replicated
Inputs may be any that keep to these rules, and one draw needn't show every extreme that they name: `labels`: values 0 to 18 name classes; 255 marks a pixel without a label.
All inputs are finite; a program needn't handle non-finite values.
Results may differ from a plain program's by a relative error of at most 0.008.
Values may be sent and summed in bfloat16 or wider, within the bound.
A program may use at most 128 MiB of HBM per device.

v0:
```python
import functools

import jax
import jax.numpy as jnp
from jax import lax
from jax.experimental import pallas as pl
from jax.experimental.pallas import tpu as pltpu
from jax.sharding import PartitionSpec as P

GROUPS = 32
NORM_FLOOR = 0.05
MESH = pl.DeviceIdType.MESH


def exchange_kernel(shape, axes, x_ref, out_ref, send_sem, recv_sem):
    coords = [lax.axis_index(axis) for axis in shape]
    names = list(shape)
    total = 1
    for axis in axes:
        total *= shape[axis]

    def peer(distance):
        ids = list(coords)
        rest = distance
        for axis in reversed(axes):
            size = shape[axis]
            ids[names.index(axis)] = lax.rem(coords[names.index(axis)] + rest % size, size)
            rest //= size
        return tuple(ids)

    barrier = pltpu.get_barrier_semaphore()
    for d in range(1, total):
        pl.semaphore_signal(barrier, inc=1, device_id=peer(d), device_id_type=MESH)
    pl.semaphore_wait(barrier, total - 1)
    copies = []
    for d in range(1, total):
        copy = pltpu.make_async_remote_copy(
            src_ref=x_ref,
            dst_ref=out_ref.at[d],
            send_sem=send_sem.at[d],
            recv_sem=recv_sem.at[d],
            device_id=peer(d),
            device_id_type=MESH,
        )
        copy.start()
        copies.append(copy)
    out_ref[0] = x_ref[...]
    for copy in copies:
        copy.wait()


def exchange(x, shape, axes, collective_id):
    total = 1
    for axis in axes:
        total *= shape[axis]
    return pl.pallas_call(
        functools.partial(exchange_kernel, shape, axes),
        out_shape=jax.ShapeDtypeStruct((total,) + x.shape, x.dtype),
        in_specs=[pl.BlockSpec(memory_space=pltpu.VMEM)],
        out_specs=pl.BlockSpec(memory_space=pltpu.VMEM),
        scratch_shapes=[pltpu.SemaphoreType.DMA((total,)), pltpu.SemaphoreType.DMA((total,))],
        compiler_params=pltpu.CompilerParams(collective_id=collective_id, has_side_effects=True),
    )(x)


def conv(framed, weight):
    return lax.conv_general_dilated(
        framed[None],
        weight,
        (1, 1),
        ((0, 0), (1, 1)),
        dimension_numbers=("NHWC", "HWIO", "NHWC"),
        preferred_element_type=jnp.float32,
    )[0]


def halo_rows(array, width):
    size, length = lax.axis_size("rows"), array.shape[0]
    before, after = [], []
    step = 1
    while width > 0:
        take = min(width, length)
        up = [(i, i + step) for i in range(size - step)]
        down = [(j, i) for i, j in up]
        before.insert(0, lax.ppermute(array[length - take :], "rows", up))
        after.append(lax.ppermute(array[:take], "rows", down))
        width -= take
        step += 1
    return before, after


def framed_by(array, width):
    before, after = halo_rows(array, width)
    return jnp.concatenate(before + [array] + after, axis=0)


def fold(values):
    return values.reshape(GROUPS, -1).sum(axis=1)


def spread(values, width):
    return jnp.repeat(values, width // GROUPS)


def double_rows(field, axis):
    count = field.shape[axis]
    first = lax.slice_in_dim(field, 0, count - 1, axis=axis)
    second = lax.slice_in_dim(field, 1, count, axis=axis)
    lines = jnp.stack([0.75 * first + 0.25 * second, 0.25 * first + 0.75 * second], axis=axis + 1)
    return lines.reshape(field.shape[:axis] + (2 * count - 2,) + field.shape[axis + 1 :])


def col_matrix(cols):
    source = lax.broadcasted_iota(jnp.int32, (cols, 2 * cols), 0)
    target = lax.broadcasted_iota(jnp.int32, (cols, 2 * cols), 1)
    near = target // 2
    far = jnp.clip(near + 2 * (target % 2) - 1, 0, cols - 1)
    return 0.75 * (source == near) + 0.25 * (source == far)


def make_per_device(shape):
    def per_device(
        feat_quarter,
        feat_eighth,
        feat_sixteenth,
        feat_thirty,
        labels,
        first_weights,
        inner_weights,
        norm_gain,
        norm_shift,
        class_weight,
        class_bias,
    ):
        position = lax.axis_index("rows")
        size = shape["rows"]

        def statistics(fields, call):
            slab, counts = [], []
            width = fields[0].shape[2]
            for y in fields:
                count = y.shape[0] * y.shape[1] * (width // GROUPS)
                sums = y.sum(axis=(0, 1))
                mean = spread(fold(sums) / count, width)
                square = (y - mean) ** 2
                slab += [sums, square.sum(axis=(0, 1))]
                counts.append(count)
            slab += [jnp.zeros_like(slab[0])] * (-len(slab) % 8)
            all_slabs = exchange(jnp.stack(slab), shape, ("rows",), call)
            folded = all_slabs.reshape(size, -1, GROUPS, width // GROUPS).sum(axis=3)
            result = []
            for i, count in enumerate(counts):
                means = folded[:, 2 * i] / count
                mean = means.mean(axis=0)
                spread_squares = count * ((means - mean) ** 2).sum(axis=0)
                var = (folded[:, 2 * i + 1].sum(axis=0) + spread_squares) / (count * size)
                result.append((mean, var))
            return result

        def activate(y, stat, layer):
            width = y.shape[2]
            factor = norm_gain[layer] * lax.rsqrt(spread(stat[1], width) + NORM_FLOOR)
            return jnp.maximum(
                (y - spread(stat[0], width)) * factor + norm_shift[layer], 0.0
            ).astype(jnp.bfloat16)

        def rows_of(count, own, extra):
            return position * own + lax.broadcasted_iota(jnp.int32, (count, 1, 1), 0) - extra

        def double(act, own, extra, kept):
            numbers = rows_of(act.shape[0], own, extra)
            top, bottom = act[extra : extra + 1], act[extra + own - 1 : extra + own]
            act = jnp.where(numbers < 0, top, jnp.where(numbers >= own * size, bottom, act))
            wide = jnp.einsum(
                "rwc,wv->rvc",
                act,
                col_matrix(act.shape[1]).astype(jnp.bfloat16),
                preferred_element_type=jnp.float32,
            )
            cut = 2 * extra - 1 - kept
            grown = double_rows(wide, 0)[cut : cut + 2 * own + 2 * kept].astype(jnp.bfloat16)
            lines = rows_of(grown.shape[0], 2 * own, kept)
            inside = (lines >= 0) & (lines < 2 * own * size)
            return jnp.where(inside, grown, jnp.zeros_like(grown))

        q, e, s, t = feat_quarter[0], feat_eighth[0], feat_sixteenth[0], feat_thirty[0]
        t_own, s_own, e_own = t.shape[0], s.shape[0], e.shape[0]
        t_framed = framed_by(t, 3)
        s_framed = framed_by(s, 2)
        e_framed = framed_by(e, 1)
        q_framed = framed_by(q, 1)
        t_out = conv(t_framed, first_weights[3])
        s_out = conv(s_framed, first_weights[2])
        t_stat, s_stat = statistics([t_out[2:-2], s_out[1:-1]], 0)
        t_out = conv(double(activate(t_out, t_stat, 3), t_own, 2, 2), inner_weights[1])
        s_out = conv(double(activate(s_out, s_stat, 2), s_own, 1, 1), inner_weights[0])
        e_out = conv(e_framed, first_weights[1])
        t_stat, s_stat, e_stat = statistics([t_out[1:-1], s_out, e_out], 1)
        s_act = activate(s_out, s_stat, 4)
        e_act = activate(e_out, e_stat, 1)
        t_out = conv(double(activate(t_out, t_stat, 5), 2 * t_own, 1, 1), inner_weights[2])
        q_out = conv(q_framed, first_weights[0])
        t_stat, q_stat = statistics([t_out, q_out], 2)
        t_act = activate(t_out, t_stat, 6)
        q_act = activate(q_out, q_stat, 0)

        coarse = jnp.einsum(
            "rwc,ck->krw",
            jnp.concatenate([e_act, s_act, t_act], axis=2),
            jnp.concatenate([class_weight] * 3, axis=0),
            preferred_element_type=jnp.float32,
        )
        up = [(i, i + 1) for i in range(size - 1)]
        down = [(j, i) for i, j in up]
        before = lax.ppermute(coarse[:, -1:], "rows", up)
        after = lax.ppermute(coarse[:, :1], "rows", down)
        before = jnp.where(position == 0, coarse[:, :1], before)
        after = jnp.where(position == size - 1, coarse[:, -1:], after)
        coarse = jnp.concatenate([before, coarse, after], axis=1)
        wide = jnp.einsum(
            "krw,wv->krv",
            coarse,
            col_matrix(coarse.shape[2]),
            precision=lax.Precision.HIGHEST,
            preferred_element_type=jnp.float32,
        )
        grown = double_rows(wide, 1)[:, 1:-1]
        scores = (
            jnp.einsum("rwc,ck->krw", q_act, class_weight, preferred_element_type=jnp.float32)
            + grown
            + class_bias[:, None, None]
        )
        log_total = jnp.log(jnp.sum(jnp.exp(scores), axis=0))
        label_map = labels[0]
        classes = jnp.arange(scores.shape[0], dtype=jnp.int32)[:, None, None]
        picked = jnp.sum(jnp.where(classes == label_map[None], scores, 0.0), axis=0)
        usable = label_map != 255
        local_total = jnp.sum(jnp.where(usable, log_total - picked, 0.0))
        local_count = jnp.sum(usable.astype(jnp.float32))
        lane = lax.broadcasted_iota(jnp.int32, (8, 128), 1)
        slab = jnp.where(lane == 0, local_total, jnp.where(lane == 1, local_count, 0.0))
        sums = exchange(slab, shape, ("batch", "rows"), 3)[:, 0].sum(axis=0)
        mean_loss = sums[0] / jnp.maximum(sums[1], 1.0)
        return (scores.astype(jnp.bfloat16)[None], mean_loss)

    return per_device


def solution(mesh):
    in_specs = (
        P("batch", "rows", None, None),
        P("batch", "rows", None, None),
        P("batch", "rows", None, None),
        P("batch", "rows", None, None),
        P("batch", "rows", None),
        P(),
        P(),
        P(),
        P(),
        P(),
        P(),
    )
    out_specs = (P("batch", None, "rows", None), P())
    return jax.shard_map(
        make_per_device(dict(mesh.shape)),
        mesh=mesh,
        in_specs=in_specs,
        out_specs=out_specs,
        check_vma=False,
    )
```

profile of v0, /device:TPU:0, one launch (start us, length us, event | category | flops | bytes accessed | tf_op | source)
XLA Modules:
  0.0 217.7 jit_solution(6644071787969341158)
XLA Ops:
  0.6 1.3 collective-permute-start.4
  1.9 5.5 %collective-permute-start.3 = (bf16[2,64,256]{2,1,0:T(8,128)(2,1)}, bf16[2,64,256]{2,1,0:T(8,128)(2,1)S(1)}, u32[]{:S(2)}, u32[]{:S(2)}) collective-permute-start(bf16[2,64,256]{2,1,0:T(8,128)(2,1)} %bitcast.253), channel_id=1, source_target_pairs={{0,1},{1,2},{2,3},{3,4},{4,5},{5,6},{6,7},{8,9},{9,10},{10,11},{11... | collective-permute-start | bytes 196616 | tf_op jit(solution)/shard_map/ppermute | solution.py:85
  7.5 0.8 slice_bitcast_fusion.24
  8.3 1.3 collective-permute-start.5
  9.6 4.6 %collective-permute-start.2 = (bf16[1,64,256]{2,1,0:T(8,128)(2,1)S(1)}, bf16[1,64,256]{2,1,0:T(8,128)(2,1)S(1)}, u32[]{:S(2)}, u32[]{:S(2)}) collective-permute-start(bf16[1,64,256]{2,1,0:T(8,128)(2,1)S(1)} %get-tuple-element.67), channel_id=1, source_target_pairs={{0,2},{1,3},{2,4},{3,5},{4,6},{5,7},{8,10},{9,11},{10,12},{11,13},... | collective-permute-start | bytes 98312 | tf_op jit(solution)/shard_map/ppermute | solution.py:85
  14.2 1.0 slice_bitcast_fusion.17
  15.2 4.8 %collective-permute-start.8 = (bf16[1,256,256]{2,1,0:T(8,128)(2,1)S(1)}, bf16[1,256,256]{2,1,0:T(8,128)(2,1)S(1)}, u32[]{:S(2)}, u32[]{:S(2)}) collective-permute-start(bf16[1,256,256]{2,1,0:T(8,128)(2,1)S(1)} %get-tuple-element.30), channel_id=1, source_target_pairs={{0,1},{1,2},{2,3},{3,4},{4,5},{5,6},{6,7},{8,9},{9,10},{10,11},{11... | collective-permute-start | bytes 393224 | tf_op jit(solution)/shard_map/ppermute | solution.py:85
  20.2 0.5 fusion.119
  20.8 0.6 fusion.115
  21.4 0.6 iota_shift-right-logical_fusion
  22.0 1.5 slice_bitcast_fusion.30
  23.5 1.0 slice_bitcast_fusion.19
  24.5 1.8 slice_bitcast_fusion.15
  26.4 1.3 collective-permute-start.9
  27.7 4.6 %collective-permute-start.6 = (bf16[2,128,256]{2,1,0:T(8,128)(2,1)S(1)}, bf16[2,128,256]{2,1,0:T(8,128)(2,1)S(1)}, u32[]{:S(2)}, u32[]{:S(2)}) collective-permute-start(bf16[2,128,256]{2,1,0:T(8,128)(2,1)S(1)} %get-tuple-element.45), channel_id=1, source_target_pairs={{0,1},{1,2},{2,3},{3,4},{4,5},{5,6},{6,7},{8,9},{9,10},{10,11},{11... | collective-permute-start | bytes 393224 | tf_op jit(solution)/shard_map/ppermute | solution.py:85
  32.3 0.8 constant_dynamic-update-slice_fusion.2
  33.1 1.3 collective-permute-start.7
  34.5 4.6 %collective-permute-start = (bf16[1,512,256]{2,1,0:T(8,128)(2,1)}, bf16[1,512,256]{2,1,0:T(8,128)(2,1)S(1)}, u32[]{:S(2)}, u32[]{:S(2)}) collective-permute-start(bf16[1,512,256]{2,1,0:T(8,128)(2,1)} %get-tuple-element.28), channel_id=1, source_target_pairs={{0,1},{1,2},{2,3},{3,4},{4,5},{5,6},{6,7},{8,9},{9,10},{10,11},{11... | collective-permute-start | bytes 786440 | tf_op jit(solution)/shard_map/ppermute | solution.py:85
  39.1 2.6 %fusion.20 = f32[1,6,64,128]{3,0,2,1:T(1,128)S(1)} fusion(bf16[4,3,3,256,128]{4,3,2,1,0:T(8,128)(2,1)} %param.16, bf16[1,8,64,256]{3,2,1,0:T(8,128)(2,1)S(1)} %bitcast.259), kind=kOutput, calls=%fused_computation.52 | convolution fusion | flops 224133120 | bytes 1048576 | tf_op jit(solution)/shard_map/conv_general_dilated | solution.py:67
  42.3 1.5 collective-permute-start.1
  43.8 4.2 %fusion.18 = f32[1,6,128,128]{3,0,2,1:T(1,128)S(1)} fusion(bf16[1,8,128,256]{3,2,1,0:T(8,128)(2,1)S(1)} %maximum_bitcast_fusion.2, bf16[4,3,3,256,128]{4,3,2,1,0:T(8,128)(2,1)} %param.16), kind=kOutput, calls=%fused_computation.31 | convolution fusion | flops 450625536 | bytes 1507328 | tf_op jit(solution)/shard_map/conv_general_dilated | solution.py:67
  48.0 0.6 fusion.166
  49.1 0.6 stack.103.x_ref
  49.7 10.9 %shard_map.122 = f32[8,8,128]{2,1,0:T(8,128)} custom-call(f32[8,128]{1,0:T(8,128)} %stack.103.x_ref), custom_call_target="tpu_custom_call" | custom-call | tf_op jit(solution)/shard_map/pallas_call | solution.py:56
  60.6 1.0 copy.48
  61.7 0.9 fusion.159
  63.7 0.8 bitcast_multiply_fusion.5
  65.1 2.5 %fusion.29 = f32[1,6,128,128]{3,0,2,1:T(1,128)S(1)} fusion(bf16[1,8,128,128]{3,2,1,0:T(8,128)(2,1)S(1)} %fusion.35, bf16[3,3,3,128,128]{4,3,2,1,0:T(8,128)(2,1)} %param.17), kind=kOutput, calls=%fused_computation.65 | convolution fusion | flops 225312768 | bytes 950272 | tf_op jit(solution)/shard_map/conv_general_dilated | solution.py:67
  67.7 0.6 fusion.165
  68.6 0.7 sub.271
  70.2 7.6 %fusion.170 = (f32[128]{0:T(128)}, f32[1,8,256,128]{3,0,2,1:T(1,128)S(1)}) fusion(bf16[3,3,3,128,128]{4,3,2,1,0:T(8,128)(2,1)} %param.17, bf16[1,10,256,128]{3,2,1,0:T(8,128)(2,1)S(1)} %bitcast_select_fusion.1), kind=kOutput, calls=%fused_computation.336 | convolution fusion | flops 602668928 | bytes 1999360 | tf_op jit(solution)/shard_map/conv_general_dilated | solution.py:67
  77.8 0.7 reshape.302
  78.5 0.7 reduce_sum.467
  79.2 0.7 broadcast_multiply_fusion.3
  80.0 0.7 sub.279
  80.9 13.9 %fusion.171 = (f32[128]{0:T(128)S(1)}, f32[1,8,256,128]{3,0,2,1:T(1,128)S(1)}) fusion(bf16[4,3,3,256,128]{4,3,2,1,0:T(8,128)(2,1)} %param.16, bf16[1,10,256,256]{3,2,1,0:T(8,128)(2,1)S(1)} %maximum_bitcast_fusion.1), kind=kOutput, calls=%fused_computation.337 | convolution fusion | flops 1205075840 | bytes 2949632 | tf_op jit(solution)/shard_map/conv_general_dilated | solution.py:67
  96.0 0.6 stack.117.x_ref
  96.6 7.8 %shard_map.123 = f32[8,8,128]{2,1,0:T(8,128)} custom-call(f32[8,128]{1,0:T(8,128)} %stack.117.x_ref), custom_call_target="tpu_custom_call" | custom-call | tf_op jit(solution)/shard_map/pallas_call | solution.py:56
  104.4 1.0 copy.56
  105.4 0.6 fusion.162
  107.1 0.5 convolution_bitcast_fusion
  108.0 6.8 %fusion.172 = (f32[128]{0:T(128)S(1)}, f32[1,8,256,128]{3,0,2,1:T(1,128)S(1)}) fusion(bf16[3,3,3,128,128]{4,3,2,1,0:T(8,128)(2,1)} %param.17, bf16[1,10,256,128]{3,2,1,0:T(8,128)(2,1)S(1)} %bitcast_select_fusion), kind=kOutput, calls=%fused_computation.338 | convolution fusion | flops 602668928 | bytes 1999360 | tf_op jit(solution)/shard_map/conv_general_dilated | solution.py:67
  116.3 2.7 %maximum_bitcast_fusion = bf16[1,18,512,256]{3,2,1,0:T(8,128)(2,1)S(1)} fusion(bf16[1,512,256]{2,1,0:T(8,128)(2,1)} %collective-permute-done.1, bf16[16,512,256]{2,1,0:T(8,128)(2,1)} %bitcast.232, bf16[1,512,256]{2,1,0:T(8,128)(2,1)S(1)} %collective-permute-done), kind=kLoop, calls=%fused_computation.2 | loop fusion | flops 4718592 | bytes 9437184 | tf_op jit(solution)/shard_map/broadcast_in_dim | solution.py:68
  119.0 48.5 %fusion.173 = (f32[128]{0:T(128)S(1)}, f32[1,16,512,128]{3,0,2,1:T(1,128)}) fusion(bf16[4,3,3,256,128]{4,3,2,1,0:T(8,128)(2,1)} %param.16, bf16[1,18,512,256]{3,2,1,0:T(8,128)(2,1)S(1)} %maximum_bitcast_fusion), kind=kOutput, calls=%fused_computation.339 | convolution fusion | flops 4826595328 | bytes 9503232 | tf_op jit(solution)/shard_map/conv_general_dilated | solution.py:67
  168.0 3.3 %multiply_reduce_fusion = f32[128]{0:T(128)S(1)} fusion(f32[16,512,128]{2,1,0:T(8,128)} %bitcast.237, f32[128]{0:T(128)S(1)} %sub.293), kind=kLoop, calls=%fused_computation.4 | loop fusion | flops 3145600 | bytes 4195328 | tf_op jit(solution)/shard_map/reduce_sum | solution.py:146
  171.3 0.6 stack.125.x_ref
  171.9 7.8 %shard_map.124 = f32[8,8,128]{2,1,0:T(8,128)} custom-call(f32[8,128]{1,0:T(8,128)} %stack.125.x_ref), custom_call_target="tpu_custom_call" | custom-call | tf_op jit(solution)/shard_map/pallas_call | solution.py:56
  179.6 1.8 copy.60
  181.4 1.1 bitcast_reduce_fusion
  182.5 0.9 fusion.164
  185.1 0.6 fusion.5
  185.8 2.6 %collective-permute-start.10 = (f32[19,1,256]{2,0,1:T(8,128)S(1)}, f32[19,1,256]{2,0,1:T(8,128)S(1)}, u32[]{:S(2)}, u32[]{:S(2)}) collective-permute-start(f32[19,1,256]{2,0,1:T(8,128)S(1)} %get-tuple-element.49), channel_id=1, source_target_pairs={{0,1},{1,2},{2,3},{3,4},{4,5},{5,6},{6,7},{8,9},{9,10},{10,11},{11... | collective-permute-start | bytes 58376 | tf_op jit(solution)/shard_map/ppermute | solution.py:215
  188.3 1.3 collective-permute-start.11
  189.9 4.3 %collective-permute-done.11 = f32[19,1,256]{2,0,1:T(8,128)S(1)} collective-permute-done((f32[19,1,256]{2,0,1:T(8,128)S(1)}, f32[19,1,256]{2,0,1:T(8,128)S(1)}, u32[]{:S(2)}, u32[]{:S(2)}) %collective-permute-start.11) | collective-permute-done | bytes 19488 | tf_op jit(solution)/shard_map/ppermute | solution.py:216
  194.2 0.7 fusion.23
  195.2 1.9 copy-done
  197.1 1.2 exponential_reduce_fusion
  198.3 0.6 select_reduce_fusion.1
  199.0 0.6 compare_select_fusion
  199.6 1.2 broadcast_select_fusion.2.x_ref
  200.9 11.8 %shard_map.125 = f32[32,8,128]{2,1,0:T(8,128)} custom-call(f32[8,128]{1,0:T(8,128)} %broadcast_select_fusion.2.x_ref), custom_call_target="tpu_custom_call" | custom-call | tf_op jit(solution)/shard_map/pallas_call | solution.py:56
  212.7 1.0 slice_reduce_fusion.7
  213.6 0.6 fusion.169
  214.2 0.8 copy.66
  (247 shorter events, 10.7 us)
Async XLA Ops:
  0.6 32.5 %collective-permute-start.4 = (bf16[2,64,256]{2,1,0:T(8,128)(2,1)}, bf16[2,64,256]{2,1,0:T(8,128)(2,1)S(1)}, u32[]{:S(2)}, u32[]{:S(2)}) collective-permute-start(bf16[2,64,256]{2,1,0:T(8,128)(2,1)} %bitcast.252), channel_id=1, source_target_pairs={{1,0},{2,1},{3,2},{4,3},{5,4},{6,5},{7,6},{9,8},{10,9},{11,10},{12... | collective-permute-start | bytes 196616 | tf_op jit(solution)/shard_map/ppermute | solution.py:86
  1.9 25.8 %collective-permute-start.3 = (bf16[2,64,256]{2,1,0:T(8,128)(2,1)}, bf16[2,64,256]{2,1,0:T(8,128)(2,1)S(1)}, u32[]{:S(2)}, u32[]{:S(2)}) collective-permute-start(bf16[2,64,256]{2,1,0:T(8,128)(2,1)} %bitcast.253), channel_id=1, source_target_pairs={{0,1},{1,2},{2,3},{3,4},{4,5},{5,6},{6,7},{8,9},{9,10},{10,11},{11... | collective-permute-start | bytes 196616 | tf_op jit(solution)/shard_map/ppermute | solution.py:85
  8.3 26.2 %collective-permute-start.5 = (bf16[1,64,256]{2,1,0:T(8,128)(2,1)S(1)}, bf16[1,64,256]{2,1,0:T(8,128)(2,1)S(1)}, u32[]{:S(2)}, u32[]{:S(2)}) collective-permute-start(bf16[1,64,256]{2,1,0:T(8,128)(2,1)S(1)} %get-tuple-element.66), channel_id=1, source_target_pairs={{2,0},{3,1},{4,2},{5,3},{6,4},{7,5},{10,8},{11,9},{12,10},{13,11},... | collective-permute-start | bytes 98312 | tf_op jit(solution)/shard_map/ppermute | solution.py:86
  9.6 16.8 %collective-permute-start.2 = (bf16[1,64,256]{2,1,0:T(8,128)(2,1)S(1)}, bf16[1,64,256]{2,1,0:T(8,128)(2,1)S(1)}, u32[]{:S(2)}, u32[]{:S(2)}) collective-permute-start(bf16[1,64,256]{2,1,0:T(8,128)(2,1)S(1)} %get-tuple-element.67), channel_id=1, source_target_pairs={{0,2},{1,3},{2,4},{3,5},{4,6},{5,7},{8,10},{9,11},{10,12},{11,13},... | collective-permute-start | bytes 98312 | tf_op jit(solution)/shard_map/ppermute | solution.py:85
  15.2 65.5 %collective-permute-start.8 = (bf16[1,256,256]{2,1,0:T(8,128)(2,1)S(1)}, bf16[1,256,256]{2,1,0:T(8,128)(2,1)S(1)}, u32[]{:S(2)}, u32[]{:S(2)}) collective-permute-start(bf16[1,256,256]{2,1,0:T(8,128)(2,1)S(1)} %get-tuple-element.30), channel_id=1, source_target_pairs={{0,1},{1,2},{2,3},{3,4},{4,5},{5,6},{6,7},{8,9},{9,10},{10,11},{11... | collective-permute-start | bytes 393224 | tf_op jit(solution)/shard_map/ppermute | solution.py:85
  20.0 49.3 %copy-start.35 = (pred[6]{0:T(512)(128)(4,1)}, pred[6]{0:T(512)(128)(4,1)S(1)}, u32[]{:S(2)}) copy-start(pred[6]{0:T(512)(128)(4,1)S(1)} %fusion.123) | copy-start | bytes 22
  20.0 49.3 %copy-start.37 = (pred[6]{0:T(512)(128)(4,1)}, pred[6]{0:T(512)(128)(4,1)S(1)}, u32[]{:S(2)}) copy-start(pred[6]{0:T(512)(128)(4,1)S(1)} %fusion.124) | copy-start | bytes 22
  20.0 49.2 %copy-start.39 = (pred[256]{0:T(512)(128)(4,1)}, pred[256]{0:T(512)(128)(4,1)S(1)}, u32[]{:S(2)}) copy-start(pred[256]{0:T(512)(128)(4,1)S(1)} %compare_and_fusion.4) | copy-start | bytes 772
  20.1 49.2 %copy-start.41 = (pred[256]{0:T(512)(128)(4,1)}, pred[256]{0:T(512)(128)(4,1)S(1)}, u32[]{:S(2)}) copy-start(pred[256]{0:T(512)(128)(4,1)S(1)} %compare_and_fusion.3) | copy-start | bytes 772
  20.2 49.1 %copy-start.25 = (s32[256]{0:T(256)}, s32[256]{0:T(256)S(1)}, u32[]{:S(2)}) copy-start(s32[256]{0:T(256)S(1)} %broadcast_add_fusion.1) | copy-start | bytes 3076
  20.2 49.1 %copy-start.27 = (s32[256]{0:T(256)}, s32[256]{0:T(256)S(1)}, u32[]{:S(2)}) copy-start(s32[256]{0:T(256)S(1)} %fusion.121) | copy-start | bytes 3076
  20.2 49.1 %copy-start.29 = (s32[256]{0:T(256)}, s32[256]{0:T(256)S(1)}, u32[]{:S(2)}) copy-start(s32[256]{0:T(256)S(1)} %iota_and_fusion.1) | copy-start | bytes 3076
  20.2 49.1 %copy-start.31 = (s32[256]{0:T(256)}, s32[256]{0:T(256)S(1)}, u32[]{:S(2)}) copy-start(s32[256]{0:T(256)S(1)} %iota_shift-right-logical_fusion.1) | copy-start | bytes 3076
  23.5 20.3 %copy-start.2 = (bf16[1,4,128,256]{3,2,1,0:T(8,128)(2,1)S(1)}, bf16[1,4,128,256]{3,2,1,0:T(8,128)(2,1)}, u32[]{:S(2)}) copy-start(bf16[1,4,128,256]{3,2,1,0:T(8,128)(2,1)} %param.13) | copy-start | bytes 786436
  26.4 43.7 %copy-start.11 = (pred[10]{0:T(512)(128)(4,1)}, pred[10]{0:T(512)(128)(4,1)S(1)}, u32[]{:S(2)}) copy-start(pred[10]{0:T(512)(128)(4,1)S(1)} %compare_and_fusion.5) | copy-start | bytes 34
  26.4 54.3 %collective-permute-start.9 = (bf16[1,256,256]{2,1,0:T(8,128)(2,1)S(1)}, bf16[1,256,256]{2,1,0:T(8,128)(2,1)S(1)}, u32[]{:S(2)}, u32[]{:S(2)}) collective-permute-start(bf16[1,256,256]{2,1,0:T(8,128)(2,1)S(1)} %get-tuple-element.31), channel_id=1, source_target_pairs={{1,0},{2,1},{3,2},{4,3},{5,4},{6,5},{7,6},{9,8},{10,9},{11,10},{12... | collective-permute-start | bytes 393224 | tf_op jit(solution)/shard_map/ppermute | solution.py:86
  27.7 14.6 %collective-permute-start.6 = (bf16[2,128,256]{2,1,0:T(8,128)(2,1)S(1)}, bf16[2,128,256]{2,1,0:T(8,128)(2,1)S(1)}, u32[]{:S(2)}, u32[]{:S(2)}) collective-permute-start(bf16[2,128,256]{2,1,0:T(8,128)(2,1)S(1)} %get-tuple-element.45), channel_id=1, source_target_pairs={{0,1},{1,2},{2,3},{3,4},{4,5},{5,6},{6,7},{8,9},{9,10},{10,11},{11... | collective-permute-start | bytes 393224 | tf_op jit(solution)/shard_map/ppermute | solution.py:85
  33.1 10.6 %collective-permute-start.7 = (bf16[2,128,256]{2,1,0:T(8,128)(2,1)S(1)}, bf16[2,128,256]{2,1,0:T(8,128)(2,1)S(1)}, u32[]{:S(2)}, u32[]{:S(2)}) collective-permute-start(bf16[2,128,256]{2,1,0:T(8,128)(2,1)S(1)} %get-tuple-element.46), channel_id=1, source_target_pairs={{1,0},{2,1},{3,2},{4,3},{5,4},{6,5},{7,6},{9,8},{10,9},{11,10},{12... | collective-permute-start | bytes 393224 | tf_op jit(solution)/shard_map/ppermute | solution.py:86
  34.5 81.8 %collective-permute-start = (bf16[1,512,256]{2,1,0:T(8,128)(2,1)}, bf16[1,512,256]{2,1,0:T(8,128)(2,1)S(1)}, u32[]{:S(2)}, u32[]{:S(2)}) collective-permute-start(bf16[1,512,256]{2,1,0:T(8,128)(2,1)} %get-tuple-element.28), channel_id=1, source_target_pairs={{0,1},{1,2},{2,3},{3,4},{4,5},{5,6},{6,7},{8,9},{9,10},{10,11},{11... | collective-permute-start | bytes 786440 | tf_op jit(solution)/shard_map/ppermute | solution.py:85
  42.3 74.0 %collective-permute-start.1 = (bf16[1,512,256]{2,1,0:T(8,128)(2,1)}, bf16[1,512,256]{2,1,0:T(8,128)(2,1)}, u32[]{:S(2)}, u32[]{:S(2)}) collective-permute-start(bf16[1,512,256]{2,1,0:T(8,128)(2,1)} %get-tuple-element.29), channel_id=1, source_target_pairs={{1,0},{2,1},{3,2},{4,3},{5,4},{6,5},{7,6},{9,8},{10,9},{11,10},{12... | collective-permute-start | bytes 786440 | tf_op jit(solution)/shard_map/ppermute | solution.py:86
  49.1 0.6 copy-start.4
  68.3 1.1 copy-start.6
  70.2 10.4 %copy-start.1 = (bf16[1,8,256,256]{3,2,1,0:T(8,128)(2,1)S(1)}, bf16[1,8,256,256]{3,2,1,0:T(8,128)(2,1)}, u32[]{:S(2)}) copy-start(bf16[1,8,256,256]{3,2,1,0:T(8,128)(2,1)} %param.12) | copy-start | bytes 3145732
  80.8 14.5 %copy-start.15 = (f32[128]{0:T(128)S(1)}, f32[128]{0:T(128)}, u32[]{:S(2)}) copy-start(f32[128]{0:T(128)} %sub.271) | copy-start | bytes 1540
  80.9 14.6 %copy-start.10 = (f32[128]{0:T(128)S(1)}, f32[128]{0:T(128)}, u32[]{:S(2)}) copy-start(f32[128]{0:T(128)} %sub.279) | copy-start | bytes 1540
  80.9 15.1 %copy-start.7 = (f32[128]{0:T(128)S(1)}, f32[128]{0:T(128)}, u32[]{:S(2)}) copy-start(f32[128]{0:T(128)} %copy-done.6) | copy-start | bytes 1540
  80.9 15.1 %copy-start.16 = (f32[128]{0:T(128)S(1)}, f32[128]{0:T(128)}, u32[]{:S(2)}) copy-start(f32[128]{0:T(128)} %get-tuple-element.83) | copy-start | bytes 1540
  94.8 11.9 %copy-start.8 = (f32[7,128]{1,0:T(8,128)S(1)}, f32[7,128]{1,0:T(8,128)}, u32[]{:S(2)}) copy-start(f32[7,128]{1,0:T(8,128)} %param.18) | copy-start | bytes 10756
  94.8 12.1 %copy-start.21 = (f32[128]{0:T(128)S(1)}, f32[128]{0:T(128)}, u32[]{:S(2)}) copy-start(f32[128]{0:T(128)} %get-tuple-element.74) | copy-start | bytes 1540
  94.8 12.2 %copy-start.26 = (s32[256]{0:T(256)S(1)}, s32[256]{0:T(256)}, u32[]{:S(2)}) copy-start(s32[256]{0:T(256)} %copy-done.25) | copy-start | bytes 3076
  94.8 12.2 %copy-start.28 = (s32[256]{0:T(256)S(1)}, s32[256]{0:T(256)}, u32[]{:S(2)}) copy-start(s32[256]{0:T(256)} %copy-done.27) | copy-start | bytes 3076
  94.8 12.2 %copy-start.30 = (s32[256]{0:T(256)S(1)}, s32[256]{0:T(256)}, u32[]{:S(2)}) copy-start(s32[256]{0:T(256)} %copy-done.29) | copy-start | bytes 3076
  94.9 12.2 %copy-start.32 = (s32[256]{0:T(256)S(1)}, s32[256]{0:T(256)}, u32[]{:S(2)}) copy-start(s32[256]{0:T(256)} %copy-done.31) | copy-start | bytes 3076
  94.9 12.2 %copy-start.36 = (pred[6]{0:T(512)(128)(4,1)S(1)}, pred[6]{0:T(512)(128)(4,1)}, u32[]{:S(2)}) copy-start(pred[6]{0:T(512)(128)(4,1)} %copy-done.35) | copy-start | bytes 22
  94.9 12.2 %copy-start.38 = (pred[6]{0:T(512)(128)(4,1)S(1)}, pred[6]{0:T(512)(128)(4,1)}, u32[]{:S(2)}) copy-start(pred[6]{0:T(512)(128)(4,1)} %copy-done.37) | copy-start | bytes 22
  94.9 12.2 %copy-start.40 = (pred[256]{0:T(512)(128)(4,1)S(1)}, pred[256]{0:T(512)(128)(4,1)}, u32[]{:S(2)}) copy-start(pred[256]{0:T(512)(128)(4,1)} %copy-done.39) | copy-start | bytes 772
  94.9 12.2 %copy-start.42 = (pred[256]{0:T(512)(128)(4,1)S(1)}, pred[256]{0:T(512)(128)(4,1)}, u32[]{:S(2)}) copy-start(pred[256]{0:T(512)(128)(4,1)} %copy-done.41) | copy-start | bytes 772
  106.9 1.0 copy-start.12
  167.5 3.7 %copy-start.5 = (f32[4,128]{1,0:T(4,128)S(1)}, f32[4,128]{1,0:T(4,128)}, u32[]{:S(2)}) copy-start(f32[4,128]{1,0:T(4,128)} %copy-done.4) | copy-start | bytes 6148
  167.9 16.4 %copy-start.9 = (f32[128]{0:T(128)S(1)}, f32[128]{0:T(128)}, u32[]{:S(2)}) copy-start(f32[128]{0:T(128)} %get-tuple-element.72) | copy-start | bytes 1540
  167.9 16.7 %copy-start.13 = (f32[128]{0:T(128)S(1)}, f32[128]{0:T(128)}, u32[]{:S(2)}) copy-start(f32[128]{0:T(128)} %get-tuple-element.77) | copy-start | bytes 1540
  168.0 16.7 %copy-start.14 = (f32[128]{0:T(128)S(1)}, f32[128]{0:T(128)}, u32[]{:S(2)}) copy-start(f32[128]{0:T(128)} %get-tuple-element.78) | copy-start | bytes 1540
  181.4 3.7 %copy-start.23 = (bf16[128,19]{0,1:T(8,128)(2,1)S(1)}, bf16[128,19]{0,1:T(8,128)(2,1)}, u32[]{:S(2)}) copy-start(bf16[128,19]{0,1:T(8,128)(2,1)} %param.20) | copy-start | bytes 14596
  184.6 9.5 %copy-start.17 = (s32[512]{0:T(512)S(1)}, s32[512]{0:T(512)}, u32[]{:S(2)}) copy-start(s32[512]{0:T(512)} %get-tuple-element.95) | copy-start | bytes 6148
  184.6 9.5 %copy-start.18 = (s32[512]{0:T(512)S(1)}, s32[512]{0:T(512)}, u32[]{:S(2)}) copy-start(s32[512]{0:T(512)} %get-tuple-element.96) | copy-start | bytes 6148
  184.6 9.5 %copy-start.19 = (s32[512]{0:T(512)S(1)}, s32[512]{0:T(512)}, u32[]{:S(2)}) copy-start(s32[512]{0:T(512)} %get-tuple-element.93) | copy-start | bytes 6148
  184.6 9.5 %copy-start.20 = (s32[512]{0:T(512)S(1)}, s32[512]{0:T(512)}, u32[]{:S(2)}) copy-start(s32[512]{0:T(512)} %get-tuple-element.94) | copy-start | bytes 6148
  184.7 9.5 %copy-start.33 = (pred[512]{0:T(512)(128)(4,1)S(1)}, pred[512]{0:T(512)(128)(4,1)}, u32[]{:S(2)}) copy-start(pred[512]{0:T(512)(128)(4,1)} %get-tuple-element.97) | copy-start | bytes 1540
  184.7 9.5 %copy-start.34 = (pred[512]{0:T(512)(128)(4,1)S(1)}, pred[512]{0:T(512)(128)(4,1)}, u32[]{:S(2)}) copy-start(pred[512]{0:T(512)(128)(4,1)} %get-tuple-element.98) | copy-start | bytes 1540
  185.8 4.1 %collective-permute-start.10 = (f32[19,1,256]{2,0,1:T(8,128)S(1)}, f32[19,1,256]{2,0,1:T(8,128)S(1)}, u32[]{:S(2)}, u32[]{:S(2)}) collective-permute-start(f32[19,1,256]{2,0,1:T(8,128)S(1)} %get-tuple-element.49), channel_id=1, source_target_pairs={{0,1},{1,2},{2,3},{3,4},{4,5},{5,6},{6,7},{8,9},{9,10},{10,11},{11... | collective-permute-start | bytes 58376 | tf_op jit(solution)/shard_map/ppermute | solution.py:215
  188.3 5.8 %collective-permute-start.11 = (f32[19,1,256]{2,0,1:T(8,128)S(1)}, f32[19,1,256]{2,0,1:T(8,128)S(1)}, u32[]{:S(2)}, u32[]{:S(2)}) collective-permute-start(f32[19,1,256]{2,0,1:T(8,128)S(1)} %get-tuple-element.50), channel_id=1, source_target_pairs={{1,0},{2,1},{3,2},{4,3},{5,4},{6,5},{7,6},{9,8},{10,9},{11,10},{12... | collective-permute-start | bytes 58376 | tf_op jit(solution)/shard_map/ppermute | solution.py:216
  194.9 2.2 %copy-start = (f32[1,16,512,128]{3,0,2,1:T(1,128)S(1)}, f32[1,16,512,128]{3,0,2,1:T(1,128)}, u32[]{:S(2)}) copy-start(f32[1,16,512,128]{3,0,2,1:T(1,128)} %get-tuple-element.90) | copy-start | bytes 12582916
  194.9 2.2 %copy-start.3 = (s32[1,16,512]{2,1,0:T(8,128)S(1)}, s32[1,16,512]{2,1,0:T(8,128)}, u32[]{:S(2)}) copy-start(s32[1,16,512]{2,1,0:T(8,128)} %param.15) | copy-start | bytes 98308
  194.9 2.2 copy-start.22
  194.9 2.2 copy-start.24
where the time goes:
time: 222 us; the launch traced here: 218 us
  matrix products  89.9 us (40%)
  Pallas kernels  38.2 us (17%)
  starting transfers between devices  34.5 us (16%)
  local copies, waits for them, and re-layouts  23.5 us (11%)
  other arithmetic  22.4 us (10%)
  between operations  4.88 us (2%)
  waiting for transfers between devices  4.3 us (2%)
    conv_general_dilated x7, matrix products, conv(): lax.conv_general_dilated(framed[None], weight, (1, 1), ((0, 0), (1, 1)),...  86.1 us
    pallas_call x4, Pallas kernels, exchange(): pl.pallas_call(functools.partial(exchange_kernel, shape, axes), out_shape...  38.2 us
    ppermute x5, starting transfers between devices, halo_rows(): before.insert(0, lax.ppermute(array[length - take:], 'rows', up))  24 us
    ppermute x5, starting transfers between devices, halo_rows(): after.append(lax.ppermute(array[:take], 'rows', down))  6.62 us
  transfers between devices with their start and end apart: 12, of which 1 were waited for; matrix products, arithmetic and copies ran while one was open for 30% of the time, Pallas kernels for 9%

commit v1 on v0

--- a/solution.py
+++ b/solution.py
@@ -63,35 +63,97 @@
     )(x)
 
 
+def conv_kernel(rows, x_ref, w_ref, y_ref, stat_ref, flat_ref):
+    cols, depth = x_ref.shape[1:]
+    width = w_ref.shape[3]
+    step = pl.program_id(0)
+
+    @pl.when(step == 0)
+    def _():
+        for down in range(3):
+            for across in range(3):
+                flat_ref[
+                    down * depth : (down + 1) * depth, across * width : (across + 1) * width
+                ] = w_ref[down, across]
+
+    lhs = jnp.concatenate(
+        [
+            x_ref[pl.ds(step * rows + down, rows)].reshape(rows * cols, depth)
+            for down in range(3)
+        ],
+        axis=1,
+    )
+    taps = jnp.dot(lhs, flat_ref[...], preferred_element_type=jnp.float32)
+    col = lax.rem(lax.broadcasted_iota(jnp.int32, (rows * cols, width), 0), cols)
+    left = jnp.where(col == 0, 0.0, pltpu.roll(taps[:, :width], 1, 0))
+    right = jnp.where(col == cols - 1, 0.0, pltpu.roll(taps[:, 2 * width :], rows * cols - 1, 0))
+    y = (taps[:, width : 2 * width] + left + right).reshape(rows, cols, width)
+    y_ref[...] = y
+    sums = jnp.sum(y, axis=1, keepdims=True)
+    centred = y - sums / cols
+    stat_ref[:, 0:1] = sums
+    stat_ref[:, 1:2] = jnp.sum(centred * centred, axis=1, keepdims=True)
+
+
 def conv(framed, weight):
-    return lax.conv_general_dilated(
-        framed[None],
-        weight,
-        (1, 1),
-        ((0, 0), (1, 1)),
-        dimension_numbers=("NHWC", "HWIO", "NHWC"),
-        preferred_element_type=jnp.float32,
-    )[0]
-
-
-def halo_rows(array, width):
-    size, length = lax.axis_size("rows"), array.shape[0]
-    before, after = [], []
+    count, cols, depth = framed.shape
+    count -= 2
+    width = weight.shape[3]
+    rows = max(r for r in range(1, count + 1) if count % r == 0 and (r == 1 or r * cols <= 1024))
+    return pl.pallas_call(
+        functools.partial(conv_kernel, rows),
+        grid=(count // rows,),
+        out_shape=(
+            jax.ShapeDtypeStruct((count, cols, width), jnp.float32),
+            jax.ShapeDtypeStruct((count, 2, width), jnp.float32),
+        ),
+        in_specs=[
+            pl.BlockSpec(framed.shape, lambda i: (0, 0, 0)),
+            pl.BlockSpec(weight.shape, lambda i: (0, 0, 0, 0)),
+        ],
+        out_specs=(
+            pl.BlockSpec((rows, cols, width), lambda i: (i, 0, 0)),
+            pl.BlockSpec((rows, 2, width), lambda i: (i, 0, 0)),
+        ),
+        scratch_shapes=[pltpu.VMEM((3 * depth, 3 * width), jnp.bfloat16)],
+        cost_estimate=pl.CostEstimate(
+            flops=18 * count * cols * depth * width,
+            bytes_accessed=2 * framed.size + 4 * count * cols * width,
+            transcendentals=0,
+        ),
+    )(framed, weight)
+
+
+def framed_by(arrays, widths):
+    size = lax.axis_size("rows")
+    lengths = [array.shape[0] for array in arrays]
+    before, after = ([[] for _ in arrays] for _ in range(2))
     step = 1
-    while width > 0:
-        take = min(width, length)
+    left = list(widths)
+    while any(left):
+        takes = [min(w, n) for w, n in zip(left, lengths)]
         up = [(i, i + step) for i in range(size - step)]
         down = [(j, i) for i, j in up]
-        before.insert(0, lax.ppermute(array[length - take :], "rows", up))
-        after.append(lax.ppermute(array[:take], "rows", down))
-        width -= take
+        for pairs, side, last in ((up, before, True), (down, after, False)):
+            parts = [
+                (a[n - k :] if last else a[:k]).reshape(-1, a.shape[2])
+                for a, n, k in zip(arrays, lengths, takes)
+                if k
+            ]
+            packed = parts[0] if len(parts) == 1 else jnp.concatenate(parts, axis=0)
+            got = lax.ppermute(packed, "rows", pairs)
+            start = 0
+            for index, (a, k) in enumerate(zip(arrays, takes)):
+                if k:
+                    end = start + k * a.shape[1]
+                    piece = got[start:end].reshape((k,) + a.shape[1:])
+                    side[index].insert(0 if last else len(side[index]), piece)
+                    start = end
+        left = [w - k for w, k in zip(left, takes)]
         step += 1
-    return before, after
-
-
-def framed_by(array, width):
-    before, after = halo_rows(array, width)
-    return jnp.concatenate(before + [array] + after, axis=0)
+    return [
+        jnp.concatenate(x + [a] + z, axis=0) for x, a, z in zip(before, arrays, after)
+    ]
 
 
 def fold(values):
@@ -135,18 +197,18 @@
         position = lax.axis_index("rows")
         size = shape["rows"]
 
-        def statistics(fields, call):
+        def statistics(fields):
             slab, counts = [], []
-            width = fields[0].shape[2]
-            for y in fields:
-                count = y.shape[0] * y.shape[1] * (width // GROUPS)
-                sums = y.sum(axis=(0, 1))
+            for rows, cols in fields:
+                width = rows.shape[2]
+                count = rows.shape[0] * cols * (width // GROUPS)
+                sums = rows[:, 0].sum(axis=0)
                 mean = spread(fold(sums) / count, width)
-                square = (y - mean) ** 2
-                slab += [sums, square.sum(axis=(0, 1))]
+                strays = cols * ((rows[:, 0] / cols - mean) ** 2).sum(axis=0)
+                slab += [sums, rows[:, 1].sum(axis=0) + strays]
                 counts.append(count)
             slab += [jnp.zeros_like(slab[0])] * (-len(slab) % 8)
-            all_slabs = exchange(jnp.stack(slab), shape, ("rows",), call)
+            all_slabs = exchange(jnp.stack(slab), shape, ("rows",), 0)
             folded = all_slabs.reshape(size, -1, GROUPS, width // GROUPS).sum(axis=3)
             result = []
             for i, count in enumerate(counts):
@@ -185,22 +247,22 @@
 
         q, e, s, t = feat_quarter[0], feat_eighth[0], feat_sixteenth[0], feat_thirty[0]
         t_own, s_own, e_own = t.shape[0], s.shape[0], e.shape[0]
-        t_framed = framed_by(t, 3)
-        s_framed = framed_by(s, 2)
-        e_framed = framed_by(e, 1)
-        q_framed = framed_by(q, 1)
-        t_out = conv(t_framed, first_weights[3])
-        s_out = conv(s_framed, first_weights[2])
-        t_stat, s_stat = statistics([t_out[2:-2], s_out[1:-1]], 0)
-        t_out = conv(double(activate(t_out, t_stat, 3), t_own, 2, 2), inner_weights[1])
-        s_out = conv(double(activate(s_out, s_stat, 2), s_own, 1, 1), inner_weights[0])
-        e_out = conv(e_framed, first_weights[1])
-        t_stat, s_stat, e_stat = statistics([t_out[1:-1], s_out, e_out], 1)
+        t_framed, s_framed = framed_by([t, s], [3, 2])
+        e_framed, q_framed = framed_by([e, q], [1, 1])
+        t_out, t_sum = conv(t_framed, first_weights[3])
+        s_out, s_sum = conv(s_framed, first_weights[2])
+        t_stat, s_stat = statistics([(t_sum[2:-2], t_out.shape[1]), (s_sum[1:-1], s_out.shape[1])])
+        t_out, t_sum = conv(double(activate(t_out, t_stat, 3), t_own, 2, 2), inner_weights[1])
+        s_out, s_sum = conv(double(activate(s_out, s_stat, 2), s_own, 1, 1), inner_weights[0])
+        e_out, e_sum = conv(e_framed, first_weights[1])
+        t_stat, s_stat, e_stat = statistics(
+            [(t_sum[1:-1], t_out.shape[1]), (s_sum, s_out.shape[1]), (e_sum, e_out.shape[1])]
+        )
         s_act = activate(s_out, s_stat, 4)
         e_act = activate(e_out, e_stat, 1)
-        t_out = conv(double(activate(t_out, t_stat, 5), 2 * t_own, 1, 1), inner_weights[2])
-        q_out = conv(q_framed, first_weights[0])
-        t_stat, q_stat = statistics([t_out, q_out], 2)
+        t_out, t_sum = conv(double(activate(t_out, t_stat, 5), 2 * t_own, 1, 1), inner_weights[2])
+        q_out, q_sum = conv(q_framed, first_weights[0])
+        t_stat, q_stat = statistics([(t_sum, t_out.shape[1]), (q_sum, q_out.shape[1])])
         t_act = activate(t_out, t_stat, 6)
         q_act = activate(q_out, q_stat, 0)
 
@@ -239,7 +301,8 @@
         local_count = jnp.sum(usable.astype(jnp.float32))
         lane = lax.broadcasted_iota(jnp.int32, (8, 128), 1)
         slab = jnp.where(lane == 0, local_total, jnp.where(lane == 1, local_count, 0.0))
-        sums = exchange(slab, shape, ("batch", "rows"), 3)[:, 0].sum(axis=0)
+        sums = exchange(slab, shape, ("rows",), 0).sum(axis=0)
+        sums = exchange(sums, shape, ("batch",), 1)[:, 0].sum(axis=0)
         mean_loss = sums[0] / jnp.maximum(sums[1], 1.0)
         return (scores.astype(jnp.bfloat16)[None], mean_loss)
 

time: 222 us -> 175 us (0.79); the launches traced: 218 us -> 173 us
  matrix products: 89.9 us -> 3.82 us
  Pallas kernels: 38.2 us -> 69.3 us
  other arithmetic: 22.4 us -> 39.4 us
  starting transfers between devices: 34.5 us -> 24.2 us
  local copies, waits for them, and re-layouts: 23.5 us -> 27.8 us
    conv_general_dilated x7 -> x0, matrix products: 86.1 us -> none  [conv(): lax.conv_general_dilated(framed[None], weight, (1, 1), ((0, 0), (1, 1)),...]
    pallas_call x0 -> x7, Pallas kernels: none -> 31.2 us  [conv(): pl.pallas_call(functools.partial(conv_kernel, rows), grid=(count // rows,...]
    ppermute x10 -> x6, starting transfers between devices: 30.6 us -> 19.5 us  [framed_by(): got = lax.ppermute(packed, 'rows', pairs)]
    concatenate x0 -> x6, other arithmetic: none -> 7.8 us  [the longest x3 6.13 us: framed_by(): jnp.concatenate(x + [a] + z, axis=0)]
    reshape x0 -> x7, local copies, waits for them, and re-layouts: none -> 5.51 us  [the longest x3 3.6 us: framed_by(): (a[n - k:] if last else a[:k]).reshape(-1, a.shape[2])]
    squeeze x0 -> x2, local copies, waits for them, and re-layouts: none -> 3.53 us  [the longest x1 2.09 us: per_device(): inner_weights[2]]
    broadcast_in_dim x4 -> x0, other arithmetic: 2.98 us -> none  [conv(): framed[None]]
    reduce_sum x8 -> x16, other arithmetic: 5.32 us -> 7.87 us  [the longest x7 5.62 us: statistics(): slab += [sums, rows[:, 1].sum(axis=0) + strays]]
  transfers between devices with their start and end apart: 12 -> 8, of which waited for: 1 -> 1; matrix products, arithmetic and copies ran while one was open for 30% -> 22% of each run, Pallas kernels for 9% -> 12%
where the time goes in v1:
time: 175 us; the launch traced here: 173 us
  Pallas kernels  69.3 us (40%)
  other arithmetic  39.4 us (23%)
  local copies, waits for them, and re-layouts  27.8 us (16%)
  starting transfers between devices  24.2 us (14%)
  between operations  4.53 us (3%)
  waiting for transfers between devices  4.22 us (2%)
  matrix products  3.82 us (2%)
    pallas_call x5, Pallas kernels, exchange(): pl.pallas_call(functools.partial(exchange_kernel, shape, axes), out_shape...  38.1 us
    pallas_call x7, Pallas kernels, conv(): pl.pallas_call(functools.partial(conv_kernel, rows), grid=(count // rows,...  31.2 us
    ppermute x6, starting transfers between devices, framed_by(): got = lax.ppermute(packed, 'rows', pairs)  19.5 us
    concatenate x3, other arithmetic, framed_by(): jnp.concatenate(x + [a] + z, axis=0)  6.13 us
    reduce_sum x7, other arithmetic, statistics(): slab += [sums, rows[:, 1].sum(axis=0) + strays]  5.62 us
    ppermute x1, waiting for transfers between devices, per_device(): after = lax.ppermute(coarse[:, :1], 'rows', down)  4.2 us
    reshape x3, local copies, waits for them, and re-layouts, framed_by(): (a[n - k:] if last else a[:k]).reshape(-1, a.shape[2])  3.6 us
    slice x4, local copies, waits for them, and re-layouts, framed_by(): piece = got[start:end].reshape((k,) + a.shape[1:])  3.52 us
  transfers between devices with their start and end apart: 8, of which 1 were waited for; matrix products, arithmetic and copies ran while one was open for 22% of the time, Pallas kernels for 12%

profile of v1, /device:TPU:0, one launch (start us, length us, event | category | flops | bytes accessed | tf_op | source)
XLA Modules:
  0.0 173.3 jit_solution(15386025105310575157)
XLA Ops:
  0.6 1.5 slice_bitcast_fusion.19
  2.2 1.3 collective-permute-start.5
  3.5 5.6 %collective-permute-start.2 = (bf16[64,256]{1,0:T(8,128)(2,1)}, bf16[64,256]{1,0:T(8,128)(2,1)S(1)}, u32[]{:S(2)}, u32[]{:S(2)}) collective-permute-start(bf16[64,256]{1,0:T(8,128)(2,1)} %get-tuple-element.110), channel_id=1, source_target_pairs={{0,2},{1,3},{2,4},{3,5},{4,6},{5,7},{8,10},{9,11},{10,12},{11,13},... | collective-permute-start | bytes 98312 | tf_op jit(solution)/shard_map/ppermute | solution.py:144
  9.1 1.0 fusion.150
  10.1 1.6 pad_maximum_fusion.9
  11.7 1.3 collective-permute-start.4
  13.0 5.2 %collective-permute-start.3 = (bf16[384,256]{1,0:T(8,128)(2,1)}, bf16[384,256]{1,0:T(8,128)(2,1)}, u32[]{:S(2)}, u32[]{:S(2)}) collective-permute-start(bf16[384,256]{1,0:T(8,128)(2,1)} %get-tuple-element.112), channel_id=1, source_target_pairs={{0,1},{1,2},{2,3},{3,4},{4,5},{5,6},{6,7},{8,9},{9,10},{10,11},{11... | collective-permute-start | bytes 589832 | tf_op jit(solution)/shard_map/ppermute | solution.py:144
  18.2 1.0 slice_bitcast_fusion.14
  19.2 1.1 slice_bitcast_fusion.10
  20.3 1.4 collective-permute-start.1
  32.8 1.5 slice_bitcast_fusion.25
  34.4 2.1 %slice_bitcast_fusion.4 = (bf16[3,3,128,128]{3,2,1,0:T(8,128)(2,1)}, bf16[3,3,128,128]{3,2,1,0:T(8,128)(2,1)}, bf16[3,3,128,128]{3,2,1,0:T(8,128)(2,1)}) fusion(bf16[3,3,3,128,128]{4,3,2,1,0:T(8,128)(2,1)} %param.17), kind=kLoop, calls=%fused_computation.63 | loop fusion | bytes 1769472 | tf_op jit(solution)/shard_map/squeeze | solution.py:263
  36.5 1.4 slice_bitcast_fusion
  38.0 4.7 %collective-permute-start = (bf16[768,256]{1,0:T(8,128)(2,1)S(1)}, bf16[768,256]{1,0:T(8,128)(2,1)S(1)}, u32[]{:S(2)}, u32[]{:S(2)}) collective-permute-start(bf16[768,256]{1,0:T(8,128)(2,1)S(1)} %pad_maximum_fusion.6), channel_id=1, source_target_pairs={{0,1},{1,2},{2,3},{3,4},{4,5},{5,6},{6,7},{8,9},{9,10},{10,11},{11... | collective-permute-start | bytes 1179656 | tf_op jit(solution)/shard_map/ppermute | solution.py:144
  42.7 0.8 slice.373
  43.7 0.9 slice.375
  44.6 0.9 slice.376
  45.6 0.9 pad_maximum_fusion.5.x_ref
  46.4 2.8 %shard_map.124 = (f32[6,128,128]{2,1,0:T(8,128)}, f32[6,2,128]{2,1,0:T(2,128)}) custom-call(bf16[8,128,256]{2,1,0:T(8,128)(2,1)} %pad_maximum_fusion.5.x_ref, bf16[3,3,256,128]{3,2,1,0:T(8,128)(2,1)} %get-tuple-element.75.w_ref), custom_call_target="tpu_custom_call" | custom-call | flops 452984832 | bytes 917504 | tf_op jit(solution)/shard_map/pallas_call | solution.py:103
  49.3 0.8 slice_reduce_fusion.17
  50.0 0.8 slice.374
  50.9 0.7 copy-done.8
  51.6 2.3 %shard_map.123 = (f32[6,64,128]{2,1,0:T(8,128)}, f32[6,2,128]{2,1,0:T(2,128)}) custom-call(bf16[8,64,256]{2,1,0:T(8,128)(2,1)} %copy-done.8, bf16[3,3,256,128]{3,2,1,0:T(8,128)(2,1)} %get-tuple-element.73.w_ref), custom_call_target="tpu_custom_call" | custom-call | flops 226492416 | bytes 458752 | tf_op jit(solution)/shard_map/pallas_call | solution.py:103
  54.0 0.8 slice_reduce_fusion.20
  56.3 9.4 %shard_map.125 = f32[8,8,128]{2,1,0:T(8,128)} custom-call(f32[8,128]{1,0:T(8,128)} %stack.87.x_ref), custom_call_target="tpu_custom_call" | custom-call | tf_op jit(solution)/shard_map/pallas_call | solution.py:56
  65.7 1.0 copy.34
  66.8 0.9 fusion.144
  68.8 1.0 maximum_convert_fusion.13
  70.4 0.8 slice_select_fusion.x_ref
  71.2 2.4 %shard_map.126 = (f32[6,128,128]{2,1,0:T(8,128)}, f32[6,2,128]{2,1,0:T(2,128)}) custom-call(bf16[8,128,128]{2,1,0:T(8,128)(2,1)} %slice_select_fusion.x_ref, bf16[3,3,128,128]{3,2,1,0:T(8,128)(2,1)} %get-tuple-element.79.w_ref), custom_call_target="tpu_custom_call" | custom-call | flops 226492416 | bytes 655360 | tf_op jit(solution)/shard_map/pallas_call | solution.py:103
  73.6 0.8 slice_reduce_fusion.16
  75.7 0.9 bitcast_select_fusion.1.x_ref
  76.6 3.4 %shard_map.127 = (f32[8,256,128]{2,1,0:T(8,128)}, f32[8,2,128]{2,1,0:T(2,128)}) custom-call(bf16[10,256,128]{2,1,0:T(8,128)(2,1)} %bitcast_select_fusion.1.x_ref, bf16[3,3,128,128]{3,2,1,0:T(8,128)(2,1)} %get-tuple-element.80.w_ref), custom_call_target="tpu_custom_call" | custom-call | flops 603979776 | bytes 1703936 | tf_op jit(solution)/shard_map/pallas_call | solution.py:103
  80.0 0.8 slice_reduce_fusion.11
  81.3 0.9 slice_bitcast_fusion.11
  82.2 1.2 pad_maximum_fusion.1.x_ref
  83.5 4.5 %shard_map.128 = (f32[8,256,128]{2,1,0:T(8,128)}, f32[8,2,128]{2,1,0:T(2,128)}) custom-call(bf16[10,256,256]{2,1,0:T(8,128)(2,1)} %pad_maximum_fusion.1.x_ref, bf16[3,3,256,128]{3,2,1,0:T(8,128)(2,1)} %get-tuple-element.72.w_ref), custom_call_target="tpu_custom_call" | custom-call | flops 1207959552 | bytes 2359296 | tf_op jit(solution)/shard_map/pallas_call | solution.py:103
  88.0 0.8 slice_reduce_fusion.10
  89.8 7.8 %shard_map.129 = f32[8,8,128]{2,1,0:T(8,128)} custom-call(f32[8,128]{1,0:T(8,128)} %stack.98.x_ref), custom_call_target="tpu_custom_call" | custom-call | tf_op jit(solution)/shard_map/pallas_call | solution.py:56
  97.6 1.0 copy.39
  101.8 0.9 bitcast_select_fusion.x_ref
  102.8 3.4 %shard_map.130 = (f32[8,256,128]{2,1,0:T(8,128)}, f32[8,2,128]{2,1,0:T(2,128)}) custom-call(bf16[10,256,128]{2,1,0:T(8,128)(2,1)} %bitcast_select_fusion.x_ref, bf16[3,3,128,128]{3,2,1,0:T(8,128)(2,1)} %get-tuple-element.78.w_ref), custom_call_target="tpu_custom_call" | custom-call | flops 603979776 | bytes 1703936 | tf_op jit(solution)/shard_map/pallas_call | solution.py:103
  106.1 0.8 slice_reduce_fusion.9
  107.4 1.0 slice_bitcast_fusion.7
  108.4 4.0 %pad_maximum_fusion.x_ref = bf16[18,512,256]{2,1,0:T(8,128)(2,1)} fusion(bf16[1,512,256]{2,1,0:T(8,128)(2,1)S(1)} %slice_bitcast_fusion.7, bf16[16,512,256]{2,1,0:T(8,128)(2,1)} %bitcast.225, bf16[1,512,256]{2,1,0:T(8,128)(2,1)S(1)} %slice_bitcast_fusion.8), kind=kLoop, calls=%fused_computation | loop fusion | flops 4718592 | bytes 9437184 | tf_op jit(solution)/shard_map/concatenate | solution.py:155
  112.4 12.4 %shard_map.122 = (f32[16,512,128]{2,1,0:T(8,128)}, f32[16,2,128]{2,1,0:T(2,128)}) custom-call(bf16[18,512,256]{2,1,0:T(8,128)(2,1)} %pad_maximum_fusion.x_ref, bf16[3,3,256,128]{3,2,1,0:T(8,128)(2,1)} %get-tuple-element.74.w_ref), custom_call_target="tpu_custom_call" | custom-call | flops 4831838208 | bytes 8912896 | tf_op jit(solution)/shard_map/pallas_call | solution.py:103
  124.8 0.9 slice_reduce_fusion.7
  126.8 7.8 %shard_map.131 = f32[8,8,128]{2,1,0:T(8,128)} custom-call(f32[8,128]{1,0:T(8,128)} %stack.104.x_ref), custom_call_target="tpu_custom_call" | custom-call | tf_op jit(solution)/shard_map/pallas_call | solution.py:56
  134.6 1.0 copy.42
  135.7 0.9 fusion.149
  137.6 1.4 maximum_convert_fusion.10
  139.5 0.6 fusion.1
  140.1 3.4 %collective-permute-start.6 = (f32[19,1,256]{2,0,1:T(8,128)S(1)}, f32[19,1,256]{2,0,1:T(8,128)S(1)}, u32[]{:S(2)}, u32[]{:S(2)}) collective-permute-start(f32[19,1,256]{2,0,1:T(8,128)S(1)} %get-tuple-element.94), channel_id=1, source_target_pairs={{0,1},{1,2},{2,3},{3,4},{4,5},{5,6},{6,7},{8,9},{9,10},{10,11},{11... | collective-permute-start | bytes 58376 | tf_op jit(solution)/shard_map/ppermute | solution.py:277
  143.6 1.3 collective-permute-start.7
  145.1 4.2 %collective-permute-done.7 = f32[19,1,256]{2,0,1:T(8,128)S(1)} collective-permute-done((f32[19,1,256]{2,0,1:T(8,128)S(1)}, f32[19,1,256]{2,0,1:T(8,128)S(1)}, u32[]{:S(2)}, u32[]{:S(2)}) %collective-permute-start.7) | collective-permute-done | bytes 19488 | tf_op jit(solution)/shard_map/ppermute | solution.py:278
  149.4 0.7 fusion.12
  150.4 1.2 exponential_reduce_fusion
  152.2 0.6 compare_select_fusion
  152.9 1.2 broadcast_select_fusion.2.x_ref
  154.1 8.2 %shard_map.132 = f32[8,8,128]{2,1,0:T(8,128)} custom-call(f32[8,128]{1,0:T(8,128)} %broadcast_select_fusion.2.x_ref), custom_call_target="tpu_custom_call" | custom-call | tf_op jit(solution)/shard_map/pallas_call | solution.py:56
  162.3 1.4 reduce_sum.578.x_ref
  163.7 5.0 %shard_map.133 = f32[4,8,128]{2,1,0:T(8,128)} custom-call(f32[8,128]{1,0:T(8,128)} %reduce_sum.578.x_ref), custom_call_target="tpu_custom_call" | custom-call | tf_op jit(solution)/shard_map/pallas_call | solution.py:56
  168.7 0.7 slice_reduce_fusion.15
  170.0 0.8 copy.48
  (259 shorter events, 24.6 us)
Async XLA Ops:
  0.6 35.8 %copy-start = (bf16[4,3,3,256,128]{4,3,2,1,0:T(8,128)(2,1)S(1)}, bf16[4,3,3,256,128]{4,3,2,1,0:T(8,128)(2,1)}, u32[]{:S(2)}) copy-start(bf16[4,3,3,256,128]{4,3,2,1,0:T(8,128)(2,1)} %param.16) | copy-start | bytes 7077892
  2.2 48.7 %collective-permute-start.5 = (bf16[64,256]{1,0:T(8,128)(2,1)}, bf16[64,256]{1,0:T(8,128)(2,1)S(1)}, u32[]{:S(2)}, u32[]{:S(2)}) collective-permute-start(bf16[64,256]{1,0:T(8,128)(2,1)} %get-tuple-element.109), channel_id=1, source_target_pairs={{2,0},{3,1},{4,2},{5,3},{6,4},{7,5},{10,8},{11,9},{12,10},{13,11},... | collective-permute-start | bytes 98312 | tf_op jit(solution)/shard_map/ppermute | solution.py:144
  3.5 34.5 %collective-permute-start.2 = (bf16[64,256]{1,0:T(8,128)(2,1)}, bf16[64,256]{1,0:T(8,128)(2,1)S(1)}, u32[]{:S(2)}, u32[]{:S(2)}) collective-permute-start(bf16[64,256]{1,0:T(8,128)(2,1)} %get-tuple-element.110), channel_id=1, source_target_pairs={{0,2},{1,3},{2,4},{3,5},{4,6},{5,7},{8,10},{9,11},{10,12},{11,13},... | collective-permute-start | bytes 98312 | tf_op jit(solution)/shard_map/ppermute | solution.py:144
  11.7 32.9 %collective-permute-start.4 = (bf16[384,256]{1,0:T(8,128)(2,1)}, bf16[384,256]{1,0:T(8,128)(2,1)}, u32[]{:S(2)}, u32[]{:S(2)}) collective-permute-start(bf16[384,256]{1,0:T(8,128)(2,1)} %get-tuple-element.111), channel_id=1, source_target_pairs={{1,0},{2,1},{3,2},{4,3},{5,4},{6,5},{7,6},{9,8},{10,9},{11,10},{12... | collective-permute-start | bytes 589832 | tf_op jit(solution)/shard_map/ppermute | solution.py:144
  13.0 29.8 %collective-permute-start.3 = (bf16[384,256]{1,0:T(8,128)(2,1)}, bf16[384,256]{1,0:T(8,128)(2,1)}, u32[]{:S(2)}, u32[]{:S(2)}) collective-permute-start(bf16[384,256]{1,0:T(8,128)(2,1)} %get-tuple-element.112), channel_id=1, source_target_pairs={{0,1},{1,2},{2,3},{3,4},{4,5},{5,6},{6,7},{8,9},{9,10},{10,11},{11... | collective-permute-start | bytes 589832 | tf_op jit(solution)/shard_map/ppermute | solution.py:144
  20.3 24.3 %copy-start.5 = (bf16[1,2,64,256]{3,2,1,0:T(8,128)(2,1)S(1)}, bf16[1,2,64,256]{3,2,1,0:T(8,128)(2,1)}, u32[]{:S(2)}) copy-start(bf16[1,2,64,256]{3,2,1,0:T(8,128)(2,1)} %param.14) | copy-start | bytes 196612
  20.3 25.2 %copy-start.4 = (bf16[1,4,128,256]{3,2,1,0:T(8,128)(2,1)S(1)}, bf16[1,4,128,256]{3,2,1,0:T(8,128)(2,1)}, u32[]{:S(2)}) copy-start(bf16[1,4,128,256]{3,2,1,0:T(8,128)(2,1)} %param.13) | copy-start | bytes 786436
  20.3 60.9 %collective-permute-start.1 = (bf16[768,256]{1,0:T(8,128)(2,1)S(1)}, bf16[768,256]{1,0:T(8,128)(2,1)}, u32[]{:S(2)}, u32[]{:S(2)}) collective-permute-start(bf16[768,256]{1,0:T(8,128)(2,1)S(1)} %pad_maximum_fusion.7), channel_id=1, source_target_pairs={{1,0},{2,1},{3,2},{4,3},{5,4},{6,5},{7,6},{9,8},{10,9},{11,10},{12... | collective-permute-start | bytes 1179656 | tf_op jit(solution)/shard_map/ppermute | solution.py:144
  37.9 30.9 %copy-start.10 = (f32[7,128]{1,0:T(8,128)S(1)}, f32[7,128]{1,0:T(8,128)}, u32[]{:S(2)}) copy-start(f32[7,128]{1,0:T(8,128)} %param.18) | copy-start | bytes 10756
  37.9 31.9 %copy-start.16 = (f32[128]{0:T(128)S(1)}, f32[128]{0:T(128)}, u32[]{:S(2)}) copy-start(f32[128]{0:T(128)} %get-tuple-element.127) | copy-start | bytes 1540
  38.0 44.2 %collective-permute-start = (bf16[768,256]{1,0:T(8,128)(2,1)S(1)}, bf16[768,256]{1,0:T(8,128)(2,1)S(1)}, u32[]{:S(2)}, u32[]{:S(2)}) collective-permute-start(bf16[768,256]{1,0:T(8,128)(2,1)S(1)} %pad_maximum_fusion.6), channel_id=1, source_target_pairs={{0,1},{1,2},{2,3},{3,4},{4,5},{5,6},{6,7},{8,9},{9,10},{10,11},{11... | collective-permute-start | bytes 1179656 | tf_op jit(solution)/shard_map/ppermute | solution.py:144
  43.6 26.3 %copy-start.19 = (pred[6]{0:T(512)(128)(4,1)S(1)}, pred[6]{0:T(512)(128)(4,1)}, u32[]{:S(2)}) copy-start(pred[6]{0:T(512)(128)(4,1)} %fusion.110) | copy-start | bytes 22
  43.6 26.3 %copy-start.20 = (pred[6]{0:T(512)(128)(4,1)S(1)}, pred[6]{0:T(512)(128)(4,1)}, u32[]{:S(2)}) copy-start(pred[6]{0:T(512)(128)(4,1)} %fusion.111) | copy-start | bytes 22
  43.6 26.3 %copy-start.21 = (s32[128]{0:T(128)S(1)}, s32[128]{0:T(128)}, u32[]{:S(2)}) copy-start(s32[128]{0:T(128)} %broadcast_add_fusion.3) | copy-start | bytes 1540
  43.6 26.3 %copy-start.22 = (s32[128]{0:T(128)S(1)}, s32[128]{0:T(128)}, u32[]{:S(2)}) copy-start(s32[128]{0:T(128)} %broadcast_add_fusion.2) | copy-start | bytes 1540
  43.6 26.3 %copy-start.23 = (s32[128]{0:T(128)S(1)}, s32[128]{0:T(128)}, u32[]{:S(2)}) copy-start(s32[128]{0:T(128)} %iota_and_fusion.2) | copy-start | bytes 1540
  43.6 26.3 %copy-start.24 = (s32[128]{0:T(128)S(1)}, s32[128]{0:T(128)}, u32[]{:S(2)}) copy-start(s32[128]{0:T(128)} %iota_shift-right-logical_fusion.2) | copy-start | bytes 1540
  43.7 26.3 %copy-start.25 = (pred[128]{0:T(512)(128)(4,1)S(1)}, pred[128]{0:T(512)(128)(4,1)}, u32[]{:S(2)}) copy-start(pred[128]{0:T(512)(128)(4,1)} %compare_and_fusion.1) | copy-start | bytes 388
  43.7 26.3 %copy-start.26 = (pred[128]{0:T(512)(128)(4,1)S(1)}, pred[128]{0:T(512)(128)(4,1)}, u32[]{:S(2)}) copy-start(pred[128]{0:T(512)(128)(4,1)} %compare_and_fusion) | copy-start | bytes 388
  49.3 20.6 %copy-start.7 = (f32[6,128,128]{2,1,0:T(8,128)S(1)}, f32[6,128,128]{2,1,0:T(8,128)}, u32[]{:S(2)}) copy-start(f32[6,128,128]{2,1,0:T(8,128)} %get-tuple-element.22) | copy-start | bytes 1179652
  49.3 21.2 %copy-start.17 = (pred[8]{0:T(512)(128)(4,1)S(1)}, pred[8]{0:T(512)(128)(4,1)}, u32[]{:S(2)}) copy-start(pred[8]{0:T(512)(128)(4,1)} %compare_and_fusion.2) | copy-start | bytes 28
  50.9 0.7 copy-start.8
  54.0 20.8 %copy-start.29 = (s32[256]{0:T(256)S(1)}, s32[256]{0:T(256)}, u32[]{:S(2)}) copy-start(s32[256]{0:T(256)} %broadcast_add_fusion.1) | copy-start | bytes 3076
  54.0 20.9 %copy-start.30 = (s32[256]{0:T(256)S(1)}, s32[256]{0:T(256)}, u32[]{:S(2)}) copy-start(s32[256]{0:T(256)} %fusion.106) | copy-start | bytes 3076
  54.0 20.9 %copy-start.31 = (s32[256]{0:T(256)S(1)}, s32[256]{0:T(256)}, u32[]{:S(2)}) copy-start(s32[256]{0:T(256)} %iota_and_fusion.1) | copy-start | bytes 3076
  54.0 20.9 %copy-start.32 = (s32[256]{0:T(256)S(1)}, s32[256]{0:T(256)}, u32[]{:S(2)}) copy-start(s32[256]{0:T(256)} %iota_shift-right-logical_fusion.1) | copy-start | bytes 3076
  54.0 20.9 %copy-start.35 = (pred[6]{0:T(512)(128)(4,1)S(1)}, pred[6]{0:T(512)(128)(4,1)}, u32[]{:S(2)}) copy-start(pred[6]{0:T(512)(128)(4,1)} %fusion.108) | copy-start | bytes 22
  54.0 20.9 %copy-start.36 = (pred[6]{0:T(512)(128)(4,1)S(1)}, pred[6]{0:T(512)(128)(4,1)}, u32[]{:S(2)}) copy-start(pred[6]{0:T(512)(128)(4,1)} %fusion.109) | copy-start | bytes 22
  54.0 20.9 %copy-start.37 = (pred[256]{0:T(512)(128)(4,1)S(1)}, pred[256]{0:T(512)(128)(4,1)}, u32[]{:S(2)}) copy-start(pred[256]{0:T(512)(128)(4,1)} %compare_and_fusion.4) | copy-start | bytes 772
  54.0 20.9 %copy-start.38 = (pred[256]{0:T(512)(128)(4,1)S(1)}, pred[256]{0:T(512)(128)(4,1)}, u32[]{:S(2)}) copy-start(pred[256]{0:T(512)(128)(4,1)} %compare_and_fusion.3) | copy-start | bytes 772
  75.4 6.8 %copy-start.1 = (bf16[1,8,256,256]{3,2,1,0:T(8,128)(2,1)S(1)}, bf16[1,8,256,256]{3,2,1,0:T(8,128)(2,1)}, u32[]{:S(2)}) copy-start(bf16[1,8,256,256]{3,2,1,0:T(8,128)(2,1)} %param.12) | copy-start | bytes 3145732
  83.4 17.5 %copy-start.6 = (f32[6,128,128]{2,1,0:T(8,128)S(1)}, f32[6,128,128]{2,1,0:T(8,128)}, u32[]{:S(2)}) copy-start(f32[6,128,128]{2,1,0:T(8,128)} %get-tuple-element.20) | copy-start | bytes 1179652
  83.4 17.5 %copy-start.15 = (f32[128]{0:T(128)S(1)}, f32[128]{0:T(128)}, u32[]{:S(2)}) copy-start(f32[128]{0:T(128)} %get-tuple-element.126) | copy-start | bytes 1540
  124.8 14.2 %copy-start.2 = (f32[8,256,128]{2,1,0:T(8,128)S(1)}, f32[8,256,128]{2,1,0:T(8,128)}, u32[]{:S(2)}) copy-start(f32[8,256,128]{2,1,0:T(8,128)} %get-tuple-element.28) | copy-start | bytes 3145732
  124.8 14.3 %copy-start.3 = (f32[8,256,128]{2,1,0:T(8,128)S(1)}, f32[8,256,128]{2,1,0:T(8,128)}, u32[]{:S(2)}) copy-start(f32[8,256,128]{2,1,0:T(8,128)} %get-tuple-element.29) | copy-start | bytes 3145732
  124.8 14.7 %copy-start.27 = (bf16[128,19]{0,1:T(8,128)(2,1)S(1)}, bf16[128,19]{0,1:T(8,128)(2,1)}, u32[]{:S(2)}) copy-start(bf16[128,19]{0,1:T(8,128)(2,1)} %param.20) | copy-start | bytes 14596
  137.5 11.8 %copy-start.11 = (s32[512]{0:T(512)S(1)}, s32[512]{0:T(512)}, u32[]{:S(2)}) copy-start(s32[512]{0:T(512)} %get-tuple-element.139) | copy-start | bytes 6148
  137.6 11.8 %copy-start.12 = (s32[512]{0:T(512)S(1)}, s32[512]{0:T(512)}, u32[]{:S(2)}) copy-start(s32[512]{0:T(512)} %get-tuple-element.140) | copy-start | bytes 6148
  137.6 11.8 %copy-start.13 = (s32[512]{0:T(512)S(1)}, s32[512]{0:T(512)}, u32[]{:S(2)}) copy-start(s32[512]{0:T(512)} %get-tuple-element.137) | copy-start | bytes 6148
  137.6 11.8 %copy-start.14 = (s32[512]{0:T(512)S(1)}, s32[512]{0:T(512)}, u32[]{:S(2)}) copy-start(s32[512]{0:T(512)} %get-tuple-element.138) | copy-start | bytes 6148
  137.6 11.8 %copy-start.33 = (pred[512]{0:T(512)(128)(4,1)S(1)}, pred[512]{0:T(512)(128)(4,1)}, u32[]{:S(2)}) copy-start(pred[512]{0:T(512)(128)(4,1)} %get-tuple-element.141) | copy-start | bytes 1540
  137.6 11.7 %copy-start.34 = (pred[512]{0:T(512)(128)(4,1)S(1)}, pred[512]{0:T(512)(128)(4,1)}, u32[]{:S(2)}) copy-start(pred[512]{0:T(512)(128)(4,1)} %get-tuple-element.142) | copy-start | bytes 1540
  140.1 10.2 %copy-start.9 = (s32[1,16,512]{2,1,0:T(8,128)S(1)}, s32[1,16,512]{2,1,0:T(8,128)}, u32[]{:S(2)}) copy-start(s32[1,16,512]{2,1,0:T(8,128)} %param.15) | copy-start | bytes 98308
  140.1 10.2 %copy-start.18 = (f32[128]{0:T(128)S(1)}, f32[128]{0:T(128)}, u32[]{:S(2)}) copy-start(f32[128]{0:T(128)} %get-tuple-element.125) | copy-start | bytes 1540
  140.1 10.2 %copy-start.28 = (f32[19]{0:T(128)S(1)}, f32[19]{0:T(128)}, u32[]{:S(2)}) copy-start(f32[19]{0:T(128)} %param.21) | copy-start | bytes 232
  140.1 4.9 %collective-permute-start.6 = (f32[19,1,256]{2,0,1:T(8,128)S(1)}, f32[19,1,256]{2,0,1:T(8,128)S(1)}, u32[]{:S(2)}, u32[]{:S(2)}) collective-permute-start(f32[19,1,256]{2,0,1:T(8,128)S(1)} %get-tuple-element.94), channel_id=1, source_target_pairs={{0,1},{1,2},{2,3},{3,4},{4,5},{5,6},{6,7},{8,9},{9,10},{10,11},{11... | collective-permute-start | bytes 58376 | tf_op jit(solution)/shard_map/ppermute | solution.py:277
  143.6 5.7 %collective-permute-start.7 = (f32[19,1,256]{2,0,1:T(8,128)S(1)}, f32[19,1,256]{2,0,1:T(8,128)S(1)}, u32[]{:S(2)}, u32[]{:S(2)}) collective-permute-start(f32[19,1,256]{2,0,1:T(8,128)S(1)} %get-tuple-element.95), channel_id=1, source_target_pairs={{1,0},{2,1},{3,2},{4,3},{5,4},{6,5},{7,6},{9,8},{10,9},{11,10},{12... | collective-permute-start | bytes 58376 | tf_op jit(solution)/shard_map/ppermute | solution.py:278
  145.1 5.3 %copy-start.39 = (f32[16,512,128]{2,1,0:T(8,128)S(1)}, f32[16,512,128]{2,1,0:T(8,128)}, u32[]{:S(2)}) copy-start(f32[16,512,128]{2,1,0:T(8,128)} %get-tuple-element.16) | copy-start | bytes 12582916

commit v2 on v1

--- a/solution.py
+++ b/solution.py
@@ -2,6 +2,7 @@
 
 import jax
 import jax.numpy as jnp
+import numpy as np
 from jax import lax
 from jax.experimental import pallas as pl
 from jax.experimental.pallas import tpu as pltpu
@@ -124,36 +125,80 @@
     )(framed, weight)
 
 
-def framed_by(arrays, widths):
-    size = lax.axis_size("rows")
-    lengths = [array.shape[0] for array in arrays]
-    before, after = ([[] for _ in arrays] for _ in range(2))
-    step = 1
-    left = list(widths)
-    while any(left):
-        takes = [min(w, n) for w, n in zip(left, lengths)]
-        up = [(i, i + step) for i in range(size - step)]
-        down = [(j, i) for i, j in up]
-        for pairs, side, last in ((up, before, True), (down, after, False)):
-            parts = [
-                (a[n - k :] if last else a[:k]).reshape(-1, a.shape[2])
-                for a, n, k in zip(arrays, lengths, takes)
-                if k
-            ]
-            packed = parts[0] if len(parts) == 1 else jnp.concatenate(parts, axis=0)
-            got = lax.ppermute(packed, "rows", pairs)
-            start = 0
-            for index, (a, k) in enumerate(zip(arrays, takes)):
-                if k:
-                    end = start + k * a.shape[1]
-                    piece = got[start:end].reshape((k,) + a.shape[1:])
-                    side[index].insert(0 if last else len(side[index]), piece)
-                    start = end
-        left = [w - k for w, k in zip(left, takes)]
-        step += 1
-    return [
-        jnp.concatenate(x + [a] + z, axis=0) for x, a, z in zip(before, arrays, after)
-    ]
+def edges_kernel(size, widths, *refs):
+    many = len(widths)
+    arrays, before, after = refs[:many], refs[many : 2 * many], refs[2 * many : 3 * many]
+    send_sem, recv_sem = refs[3 * many :]
+    me = lax.axis_index("rows")
+    reach = max(-(-w // a.shape[0]) for a, w in zip(arrays, widths))
+    barrier = pltpu.get_barrier_semaphore()
+    sides = [side * step for step in range(1, reach + 1) for side in (1, -1)]
+
+    def exists(offset):
+        return me + offset < size if offset > 0 else me + offset >= 0
+
+    def target(offset):
+        return {"rows": lax.rem(me + offset + size, size)}
+
+    for offset in sides:
+
+        @pl.when(exists(offset))
+        def _():
+            pl.semaphore_signal(
+                barrier, inc=1, device_id=target(offset), device_id_type=MESH
+            )
+
+    peers = jnp.minimum(me, reach) + jnp.minimum(size - 1 - me, reach)
+    pl.semaphore_wait(barrier, peers)
+
+    copies = []
+    for index in reversed(range(many)):
+        array, width = arrays[index], widths[index]
+        length = array.shape[0]
+        done, step = 0, 1
+        while done < width:
+            take = min(width - done, length)
+            for offset in (step, -step):
+                if offset > 0:
+                    source = array.at[length - take : length]
+                    landing = before[index].at[width - done - take : width - done]
+                else:
+                    source = array.at[0:take]
+                    landing = after[index].at[done : done + take]
+                copy = pltpu.make_async_remote_copy(
+                    src_ref=source,
+                    dst_ref=landing,
+                    send_sem=send_sem.at[len(copies)],
+                    recv_sem=recv_sem.at[len(copies)],
+                    device_id=target(offset),
+                    device_id_type=MESH,
+                )
+                copies.append((copy, offset, landing))
+                pl.when(exists(offset))(copy.start)
+            done += take
+            step += 1
+    for copy, offset, landing in copies:
+
+        @pl.when(jnp.logical_not(exists(-offset)))
+        def _():
+            landing[...] = jnp.zeros(landing.shape, landing.dtype)
+
+        pl.when(exists(offset))(copy.wait_send)
+        pl.when(exists(-offset))(copy.wait_recv)
+
+
+def edges(arrays, widths, size, collective_id):
+    outs = [jax.ShapeDtypeStruct((w,) + a.shape[1:], a.dtype) for a, w in zip(arrays, widths)]
+    copies = 2 * sum(-(-w // a.shape[0]) for a, w in zip(arrays, widths))
+    got = pl.pallas_call(
+        functools.partial(edges_kernel, size, tuple(widths)),
+        out_shape=tuple(outs + outs),
+        in_specs=[pl.BlockSpec(memory_space=pl.ANY)] * len(arrays),
+        out_specs=tuple([pl.BlockSpec(memory_space=pltpu.VMEM)] * (2 * len(arrays))),
+        scratch_shapes=[pltpu.SemaphoreType.DMA((copies,)), pltpu.SemaphoreType.DMA((copies,))],
+        compiler_params=pltpu.CompilerParams(collective_id=collective_id, has_side_effects=True),
+    )(*arrays)
+    return got[: len(arrays)], got[len(arrays) :]
 
 
 def fold(values):
@@ -173,11 +218,11 @@
 
 
 def col_matrix(cols):
-    source = lax.broadcasted_iota(jnp.int32, (cols, 2 * cols), 0)
-    target = lax.broadcasted_iota(jnp.int32, (cols, 2 * cols), 1)
+    target = np.arange(2 * cols)
     near = target // 2
-    far = jnp.clip(near + 2 * (target % 2) - 1, 0, cols - 1)
-    return 0.75 * (source == near) + 0.25 * (source == far)
+    far = np.clip(near + 2 * (target % 2) - 1, 0, cols - 1)
+    source = np.arange(cols)[:, None]
+    return (0.75 * (source == near) + 0.25 * (source == far)).astype(np.float32)
 
 
 def make_per_device(shape):
@@ -226,29 +271,32 @@
                 (y - spread(stat[0], width)) * factor + norm_shift[layer], 0.0
             ).astype(jnp.bfloat16)
 
-        def rows_of(count, own, extra):
-            return position * own + lax.broadcasted_iota(jnp.int32, (count, 1, 1), 0) - extra
+        def rows_of(dims, own, extra):
+            return position * own + lax.broadcasted_iota(jnp.int32, dims, 0) - extra
 
         def double(act, own, extra, kept):
-            numbers = rows_of(act.shape[0], own, extra)
+            numbers = rows_of(act.shape, own, extra)
             top, bottom = act[extra : extra + 1], act[extra + own - 1 : extra + own]
             act = jnp.where(numbers < 0, top, jnp.where(numbers >= own * size, bottom, act))
             wide = jnp.einsum(
                 "rwc,wv->rvc",
                 act,
-                col_matrix(act.shape[1]).astype(jnp.bfloat16),
+                jnp.asarray(col_matrix(act.shape[1]), jnp.bfloat16),
                 preferred_element_type=jnp.float32,
             )
             cut = 2 * extra - 1 - kept
             grown = double_rows(wide, 0)[cut : cut + 2 * own + 2 * kept].astype(jnp.bfloat16)
-            lines = rows_of(grown.shape[0], 2 * own, kept)
+            lines = rows_of(grown.shape, 2 * own, kept)
             inside = (lines >= 0) & (lines < 2 * own * size)
             return jnp.where(inside, grown, jnp.zeros_like(grown))
 
         q, e, s, t = feat_quarter[0], feat_eighth[0], feat_sixteenth[0], feat_thirty[0]
         t_own, s_own, e_own = t.shape[0], s.shape[0], e.shape[0]
-        t_framed, s_framed = framed_by([t, s], [3, 2])
-        e_framed, q_framed = framed_by([e, q], [1, 1])
+        bands = [q, e, s, t]
+        q_framed, e_framed, s_framed, t_framed = [
+            jnp.concatenate([x, band, z], axis=0)
+            for x, band, z in zip(*((lambda g: (g[0], bands, g[1]))(edges(bands, [1, 1, 2, 3], size, 2))))
+        ]
         t_out, t_sum = conv(t_framed, first_weights[3])
         s_out, s_sum = conv(s_framed, first_weights[2])
         t_stat, s_stat = statistics([(t_sum[2:-2], t_out.shape[1]), (s_sum[1:-1], s_out.shape[1])])
@@ -267,18 +315,15 @@
         q_act = activate(q_out, q_stat, 0)
 
         coarse = jnp.einsum(
-            "rwc,ck->krw",
+            "rwc,ck->rkw",
             jnp.concatenate([e_act, s_act, t_act], axis=2),
             jnp.concatenate([class_weight] * 3, axis=0),
             preferred_element_type=jnp.float32,
         )
-        up = [(i, i + 1) for i in range(size - 1)]
-        down = [(j, i) for i, j in up]
-        before = lax.ppermute(coarse[:, -1:], "rows", up)
-        after = lax.ppermute(coarse[:, :1], "rows", down)
-        before = jnp.where(position == 0, coarse[:, :1], before)
-        after = jnp.where(position == size - 1, coarse[:, -1:], after)
-        coarse = jnp.concatenate([before, coarse, after], axis=1)
+        (before,), (after,) = edges([coarse], [1], size, 3)
+        before = jnp.where(position == 0, coarse[:1], before)
+        after = jnp.where(position == size - 1, coarse[-1:], after)
+        coarse = jnp.concatenate([before, coarse, after], axis=0).transpose(1, 0, 2)
         wide = jnp.einsum(
             "krw,wv->krv",
             coarse,

time: 175 us -> 164 us (0.937)
  Pallas kernels: 69.3 us -> 104 us
  starting transfers between devices: 24.2 us -> 0 us
  local copies, waits for them, and re-layouts: 27.8 us -> 17.4 us
  other arithmetic: 39.4 us -> 31.2 us
  waiting for transfers between devices: 4.22 us -> 0 us
    pallas_call x0 -> x2, Pallas kernels: none -> 34.9 us  [edges(): pl.pallas_call(functools.partial(edges_kernel, size, tuple(widths)), out_...]
    ppermute x8 -> x0, starting transfers between devices: 24.2 us -> none  [the longest x6 19.5 us: framed_by(): got = lax.ppermute(packed, 'rows', pairs)]
    reshape x7 -> x0, local copies, waits for them, and re-layouts: 5.51 us -> none  [the longest x3 3.6 us: framed_by(): (a[n - k:] if last else a[:k]).reshape(-1, a.shape[2])]
    slice x6 -> x0, local copies, waits for them, and re-layouts: 4.51 us -> none  [the longest x4 3.52 us: framed_by(): piece = got[start:end].reshape((k,) + a.shape[1:])]
    ppermute x8 -> x0, waiting for transfers between devices: 4.22 us -> none  [the longest x1 4.2 us: per_device(): after = lax.ppermute(coarse[:, :1], 'rows', down)]
    and x5 -> x0, other arithmetic: 2.62 us -> none  [the longest x3 1.56 us: col_matrix(): near = target // 2]
    concatenate x6 -> x4, other arithmetic: 7.8 us -> 9.91 us  [per_device(): jnp.concatenate([x, band, z], axis=0)]
    add x3 -> x0, other arithmetic: 1.77 us -> none  [col_matrix(): far = jnp.clip(near + 2 * (target % 2) - 1, 0, cols - 1)]
  transfers between devices with their start and end apart: 8 -> 0, of which waited for: 1 -> 0; matrix products, arithmetic and copies ran while one was open for 22% -> 0% of each run, Pallas kernels for 12% -> 0%
where the time goes in v2:
time: 164 us; the launch traced here: 162 us
  Pallas kernels  104 us (63%)
  other arithmetic  31.2 us (19%)
  local copies, waits for them, and re-layouts  17.4 us (11%)
  matrix products  5.34 us (3%)
  between operations  3.99 us (2%)
    pallas_call x5, Pallas kernels, exchange(): pl.pallas_call(functools.partial(exchange_kernel, shape, axes), out_shape...  38.3 us
    pallas_call x2, Pallas kernels, edges(): pl.pallas_call(functools.partial(edges_kernel, size, tuple(widths)), out_...  34.9 us
    pallas_call x7, Pallas kernels, conv(): pl.pallas_call(functools.partial(conv_kernel, rows), grid=(count // rows,...  31.2 us
    concatenate x4, other arithmetic, per_device(): jnp.concatenate([x, band, z], axis=0)  9.91 us
    reduce_sum x7, other arithmetic, statistics(): slab += [sums, rows[:, 1].sum(axis=0) + strays]  5.59 us

profile of v2, /device:TPU:0, one launch (start us, length us, event | category | flops | bytes accessed | tf_op | source)
XLA Modules:
  0.0 162.3 jit_solution(16644040151989144967)
XLA Ops:
  0.7 0.9 slice_bitcast_fusion.15
  1.7 2.1 %slice_bitcast_fusion.4 = (bf16[3,3,128,128]{3,2,1,0:T(8,128)(2,1)}, bf16[3,3,128,128]{3,2,1,0:T(8,128)(2,1)}, bf16[3,3,128,128]{3,2,1,0:T(8,128)(2,1)}) fusion(bf16[3,3,3,128,128]{4,3,2,1,0:T(8,128)(2,1)} %param.21), kind=kLoop, calls=%fused_computation.52 | loop fusion | bytes 1769472 | tf_op jit(solution)/shard_map/squeeze | solution.py:311
  3.8 29.9 %shard_map.158 = (bf16[1,512,256]{2,1,0:T(8,128)(2,1)}, bf16[1,256,256]{2,1,0:T(8,128)(2,1)}, bf16[2,128,256]{2,1,0:T(8,128)(2,1)}, bf16[3,64,256]{2,1,0:T(8,128...) custom-call(bf16[16,512,256]{2,1,0:T(8,128)(2,1)} %bitcast.195, ...), custom_call_target="tpu_custom_call" | custom-call | tf_op jit(solution)/shard_map/pallas_call | solution.py:193
  33.7 1.8 %pad_maximum_fusion.7.x_ref = bf16[8,64,256]{2,1,0:T(8,128)(2,1)} fusion(bf16[3,64,256]{2,1,0:T(8,128)(2,1)} %get-tuple-element.30, bf16[2,64,256]{2,1,0:T(8,128)(2,1)S(1)} %bitcast.204, bf16[3,64,256]{2,1,0:T(8,128)(2,1)} %get-tuple-element.29), kind=kLoop, calls=%fused_computation.56 | loop fusion | flops 262144 | bytes 524288 | tf_op jit(solution)/shard_map/concatenate | solution.py:297
  35.5 1.9 %pad_maximum_fusion.5.x_ref = bf16[8,128,256]{2,1,0:T(8,128)(2,1)} fusion(bf16[2,128,256]{2,1,0:T(8,128)(2,1)} %get-tuple-element.34, bf16[4,128,256]{2,1,0:T(8,128)(2,1)S(1)} %bitcast.201, bf16[2,128,256]{2,1,0:T(8,128)(2,1)} %get-tuple-element.33), kind=kLoop, calls=%fused_computation.36 | loop fusion | flops 524288 | bytes 1048576 | tf_op jit(solution)/shard_map/concatenate | solution.py:297
  37.4 2.2 %pad_maximum_fusion.1.x_ref = bf16[10,256,256]{2,1,0:T(8,128)(2,1)} fusion(bf16[1,256,256]{2,1,0:T(8,128)(2,1)} %get-tuple-element.41, bf16[8,256,256]{2,1,0:T(8,128)(2,1)S(1)} %bitcast.198, bf16[1,256,256]{2,1,0:T(8,128)(2,1)} %get-tuple-element.40), kind=kLoop, calls=%fused_computation.9 | loop fusion | flops 1310720 | bytes 2621440 | tf_op jit(solution)/shard_map/concatenate | solution.py:297
  39.6 1.4 slice_bitcast_fusion
  41.0 2.8 %shard_map.161 = (f32[6,128,128]{2,1,0:T(8,128)}, f32[6,2,128]{2,1,0:T(2,128)}) custom-call(bf16[8,128,256]{2,1,0:T(8,128)(2,1)} %pad_maximum_fusion.5.x_ref, bf16[3,3,256,128]{3,2,1,0:T(8,128)(2,1)} %get-tuple-element.93.w_ref), custom_call_target="tpu_custom_call" | custom-call | flops 452984832 | bytes 917504 | tf_op jit(solution)/shard_map/pallas_call | solution.py:104
  43.8 0.8 slice_reduce_fusion.17
  44.6 4.5 %shard_map.165 = (f32[8,256,128]{2,1,0:T(8,128)}, f32[8,2,128]{2,1,0:T(2,128)}) custom-call(bf16[10,256,256]{2,1,0:T(8,128)(2,1)} %pad_maximum_fusion.1.x_ref, bf16[3,3,256,128]{3,2,1,0:T(8,128)(2,1)} %get-tuple-element.90.w_ref), custom_call_target="tpu_custom_call" | custom-call | flops 1207959552 | bytes 2359296 | tf_op jit(solution)/shard_map/pallas_call | solution.py:104
  49.1 2.4 %shard_map.160 = (f32[6,64,128]{2,1,0:T(8,128)}, f32[6,2,128]{2,1,0:T(2,128)}) custom-call(bf16[8,64,256]{2,1,0:T(8,128)(2,1)} %pad_maximum_fusion.7.x_ref, bf16[3,3,256,128]{3,2,1,0:T(8,128)(2,1)} %get-tuple-element.91.w_ref), custom_call_target="tpu_custom_call" | custom-call | flops 226492416 | bytes 458752 | tf_op jit(solution)/shard_map/pallas_call | solution.py:104
  51.5 0.8 slice_reduce_fusion.10
  52.3 0.8 slice_reduce_fusion.20
  54.4 0.6 stack.87.x_ref
  55.0 9.7 %shard_map.162 = f32[8,8,128]{2,1,0:T(8,128)} custom-call(f32[8,128]{1,0:T(8,128)} %stack.87.x_ref), custom_call_target="tpu_custom_call" | custom-call | tf_op jit(solution)/shard_map/pallas_call | solution.py:57
  64.7 1.0 copy.44
  65.8 0.9 fusion.69
  66.9 0.1 copy.45
  67.7 1.0 maximum_convert_fusion.13
  68.9 0.3 convolution_bitcast_fusion.2
  69.4 0.2 copy.46
  69.6 0.8 slice_select_fusion.x_ref
  70.4 2.4 %shard_map.163 = (f32[6,128,128]{2,1,0:T(8,128)}, f32[6,2,128]{2,1,0:T(2,128)}) custom-call(bf16[8,128,128]{2,1,0:T(8,128)(2,1)} %slice_select_fusion.x_ref, bf16[3,3,128,128]{3,2,1,0:T(8,128)(2,1)} %get-tuple-element.95.w_ref), custom_call_target="tpu_custom_call" | custom-call | flops 226492416 | bytes 655360 | tf_op jit(solution)/shard_map/pallas_call | solution.py:104
  72.8 0.8 slice_reduce_fusion.16
  74.0 0.4 convolution_bitcast_fusion.1
  74.4 0.1 fusion.13
  74.6 0.3 copy.49
  74.9 0.9 bitcast_select_fusion.1.x_ref
  75.9 3.4 %shard_map.164 = (f32[8,256,128]{2,1,0:T(8,128)}, f32[8,2,128]{2,1,0:T(2,128)}) custom-call(bf16[10,256,128]{2,1,0:T(8,128)(2,1)} %bitcast_select_fusion.1.x_ref, bf16[3,3,128,128]{3,2,1,0:T(8,128)(2,1)} %get-tuple-element.96.w_ref), custom_call_target="tpu_custom_call" | custom-call | flops 603979776 | bytes 1703936 | tf_op jit(solution)/shard_map/pallas_call | solution.py:104
  79.3 0.8 slice_reduce_fusion.11
  80.5 0.6 stack.98.x_ref
  81.2 7.8 %shard_map.166 = f32[8,8,128]{2,1,0:T(8,128)} custom-call(f32[8,128]{1,0:T(8,128)} %stack.98.x_ref), custom_call_target="tpu_custom_call" | custom-call | tf_op jit(solution)/shard_map/pallas_call | solution.py:57
  88.9 1.0 copy.50
  90.0 0.6 fusion.72
  90.8 0.1 copy.57
  92.3 0.4 convolution_bitcast_fusion
  93.0 0.3 copy.53
  93.3 1.0 bitcast_select_fusion.x_ref
  94.2 3.4 %shard_map.167 = (f32[8,256,128]{2,1,0:T(8,128)}, f32[8,2,128]{2,1,0:T(2,128)}) custom-call(bf16[10,256,128]{2,1,0:T(8,128)(2,1)} %bitcast_select_fusion.x_ref, bf16[3,3,128,128]{3,2,1,0:T(8,128)(2,1)} %get-tuple-element.94.w_ref), custom_call_target="tpu_custom_call" | custom-call | flops 603979776 | bytes 1703936 | tf_op jit(solution)/shard_map/pallas_call | solution.py:104
  97.6 0.8 slice_reduce_fusion.9
  98.9 4.0 %pad_maximum_fusion.x_ref = bf16[18,512,256]{2,1,0:T(8,128)(2,1)} fusion(bf16[1,512,256]{2,1,0:T(8,128)(2,1)S(1)} %copy-done.10, bf16[16,512,256]{2,1,0:T(8,128)(2,1)} %bitcast.196, bf16[1,512,256]{2,1,0:T(8,128)(2,1)S(1)} %copy-done.9), kind=kLoop, calls=%fused_computation | loop fusion | flops 4718592 | bytes 9437184 | tf_op jit(solution)/shard_map/concatenate | solution.py:297
  102.9 12.4 %shard_map.159 = (f32[16,512,128]{2,1,0:T(8,128)}, f32[16,2,128]{2,1,0:T(2,128)}) custom-call(bf16[18,512,256]{2,1,0:T(8,128)(2,1)} %pad_maximum_fusion.x_ref, bf16[3,3,256,128]{3,2,1,0:T(8,128)(2,1)} %get-tuple-element.92.w_ref), custom_call_target="tpu_custom_call" | custom-call | flops 4831838208 | bytes 8912896 | tf_op jit(solution)/shard_map/pallas_call | solution.py:104
  115.3 0.9 slice_reduce_fusion.7
  116.7 0.6 stack.104.x_ref
  117.3 7.8 %shard_map.168 = f32[8,8,128]{2,1,0:T(8,128)} custom-call(f32[8,128]{1,0:T(8,128)} %stack.104.x_ref), custom_call_target="tpu_custom_call" | custom-call | tf_op jit(solution)/shard_map/pallas_call | solution.py:57
  125.1 1.0 copy.54
  126.1 0.9 fusion.74
  128.0 1.4 maximum_convert_fusion.10
  129.6 0.4 maximum_convert_fusion.8
  130.0 1.4 fusion.10.refs_0_
  131.4 5.0 %shard_map.169 = (f32[1,19,256]{2,1,0:T(8,128)}, f32[1,19,256]{2,1,0:T(8,128)}) custom-call(f32[8,19,256]{2,1,0:T(8,128)} %fusion.10.refs_0_), custom_call_target="tpu_custom_call" | custom-call | tf_op jit(solution)/shard_map/pallas_call | solution.py:193
  136.4 0.8 slice_select_fusion.2
  137.3 1.7 %fusion.17 = f32[19,10,512]{2,0,1:T(8,128)S(1)} fusion(f32[256,512,1]{1,0,2:T(8,128)S(1)} %copy-done.5, f32[1,19,256]{2,1,0:T(8,128)S(1)} %get-tuple-element.107, f32[8,19,256]{2,1,0:T(8,128)} %fusion.10.refs_0_, f32[1,19,256]{2,1,0:T(8,128)S(1)} %get-tuple-element.106), kind=kOutput, calls=%fused_computation.58 | convolution fusion | flops 298941440 | bytes 1107968 | tf_op jit(solution)/shard_map/krw,wv->krv/dot_general | solution.py:327
  139.2 0.3 copy-done.17
  139.5 1.2 exponential_reduce_fusion
  140.8 0.6 select_reduce_fusion.1
  141.4 0.6 compare_select_fusion
  142.1 1.2 broadcast_select_fusion.x_ref
  143.3 8.1 %shard_map.170 = f32[8,8,128]{2,1,0:T(8,128)} custom-call(f32[8,128]{1,0:T(8,128)} %broadcast_select_fusion.x_ref), custom_call_target="tpu_custom_call" | custom-call | tf_op jit(solution)/shard_map/pallas_call | solution.py:57
  151.4 1.4 reduce_sum.578.x_ref
  152.8 5.0 %shard_map.171 = f32[4,8,128]{2,1,0:T(8,128)} custom-call(f32[8,128]{1,0:T(8,128)} %reduce_sum.578.x_ref), custom_call_target="tpu_custom_call" | custom-call | tf_op jit(solution)/shard_map/pallas_call | solution.py:57
  157.8 0.7 slice_reduce_fusion.15
  158.5 0.6 fusion.75
  160.4 0.8 copy.60
  (166 shorter events, 7.5 us)
Async XLA Ops:
  3.7 29.9 %copy-start.8 = (bf16[1,2,64,256]{3,2,1,0:T(8,128)(2,1)S(1)}, bf16[1,2,64,256]{3,2,1,0:T(8,128)(2,1)}, u32[]{:S(2)}) copy-start(bf16[1,2,64,256]{3,2,1,0:T(8,128)(2,1)} %param.18) | copy-start | bytes 196612
  3.8 31.8 %copy-start.4 = (bf16[1,4,128,256]{3,2,1,0:T(8,128)(2,1)S(1)}, bf16[1,4,128,256]{3,2,1,0:T(8,128)(2,1)}, u32[]{:S(2)}) copy-start(bf16[1,4,128,256]{3,2,1,0:T(8,128)(2,1)} %param.17) | copy-start | bytes 786436
  3.8 33.6 %copy-start = (bf16[1,8,256,256]{3,2,1,0:T(8,128)(2,1)S(1)}, bf16[1,8,256,256]{3,2,1,0:T(8,128)(2,1)}, u32[]{:S(2)}) copy-start(bf16[1,8,256,256]{3,2,1,0:T(8,128)(2,1)} %param.16) | copy-start | bytes 3145732
  33.7 5.9 %copy-start.1 = (bf16[4,3,3,256,128]{4,3,2,1,0:T(8,128)(2,1)S(1)}, bf16[4,3,3,256,128]{4,3,2,1,0:T(8,128)(2,1)}, u32[]{:S(2)}) copy-start(bf16[4,3,3,256,128]{4,3,2,1,0:T(8,128)(2,1)} %param.20) | copy-start | bytes 7077892
  44.6 23.1 %copy-start.14 = (f32[7,128]{1,0:T(8,128)S(1)}, f32[7,128]{1,0:T(8,128)}, u32[]{:S(2)}) copy-start(f32[7,128]{1,0:T(8,128)} %param.22) | copy-start | bytes 10756
  44.6 24.2 %copy-start.6 = (f32[6,128,128]{2,1,0:T(8,128)S(1)}, f32[6,128,128]{2,1,0:T(8,128)}, u32[]{:S(2)}) copy-start(f32[6,128,128]{2,1,0:T(8,128)} %get-tuple-element.38) | copy-start | bytes 1179652
  49.1 19.8 %copy-start.13 = (bf16[64,128,1]{1,0,2:T(8,128)(2,1)S(1)}, bf16[64,128,1]{1,0,2:T(8,128)(2,1)}, u32[]{:S(2)}) copy-start(bf16[64,128,1]{1,0,2:T(8,128)(2,1)} %constant.153) | copy-start | bytes 49156
  65.8 8.2 %copy-start.11 = (bf16[128,256,1]{1,0,2:T(8,128)(2,1)S(1)}, bf16[128,256,1]{1,0,2:T(8,128)(2,1)}, u32[]{:S(2)}) copy-start(bf16[128,256,1]{1,0,2:T(8,128)(2,1)} %constant.154) | copy-start | bytes 196612
  74.9 16.6 %copy-start.7 = (f32[6,128,128]{2,1,0:T(8,128)S(1)}, f32[6,128,128]{2,1,0:T(8,128)}, u32[]{:S(2)}) copy-start(f32[6,128,128]{2,1,0:T(8,128)} %get-tuple-element.36) | copy-start | bytes 1179652
  92.9 6.0 %copy-start.9 = (bf16[1,512,256]{2,1,0:T(8,128)(2,1)S(1)}, bf16[1,512,256]{2,1,0:T(8,128)(2,1)}, u32[]{:S(2)}) copy-start(bf16[1,512,256]{2,1,0:T(8,128)(2,1)} %get-tuple-element.26) | copy-start | bytes 786436
  92.9 6.0 %copy-start.10 = (bf16[1,512,256]{2,1,0:T(8,128)(2,1)S(1)}, bf16[1,512,256]{2,1,0:T(8,128)(2,1)}, u32[]{:S(2)}) copy-start(bf16[1,512,256]{2,1,0:T(8,128)(2,1)} %get-tuple-element.27) | copy-start | bytes 786436
  115.3 14.3 %copy-start.2 = (f32[8,256,128]{2,1,0:T(8,128)S(1)}, f32[8,256,128]{2,1,0:T(8,128)}, u32[]{:S(2)}) copy-start(f32[8,256,128]{2,1,0:T(8,128)} %get-tuple-element.46) | copy-start | bytes 3145732
  115.3 14.3 %copy-start.3 = (f32[8,256,128]{2,1,0:T(8,128)S(1)}, f32[8,256,128]{2,1,0:T(8,128)}, u32[]{:S(2)}) copy-start(f32[8,256,128]{2,1,0:T(8,128)} %get-tuple-element.47) | copy-start | bytes 3145732
  126.1 3.9 %copy-start.15 = (bf16[128,19]{0,1:T(8,128)(2,1)S(1)}, bf16[128,19]{0,1:T(8,128)(2,1)}, u32[]{:S(2)}) copy-start(bf16[128,19]{0,1:T(8,128)(2,1)} %param.24) | copy-start | bytes 14596
  129.6 7.6 %copy-start.5 = (f32[256,512,1]{1,0,2:T(8,128)S(1)}, f32[256,512,1]{1,0,2:T(8,128)}, u32[]{:S(2)}) copy-start(f32[256,512,1]{1,0,2:T(8,128)} %constant.155) | copy-start | bytes 1572868
  137.2 2.0 %copy-start.12 = (s32[1,16,512]{2,1,0:T(8,128)S(1)}, s32[1,16,512]{2,1,0:T(8,128)}, u32[]{:S(2)}) copy-start(s32[1,16,512]{2,1,0:T(8,128)} %param.19) | copy-start | bytes 98308
  137.2 2.0 %copy-start.16 = (f32[19]{0:T(128)S(1)}, f32[19]{0:T(128)}, u32[]{:S(2)}) copy-start(f32[19]{0:T(128)} %param.25) | copy-start | bytes 232
  137.2 2.3 %copy-start.17 = (f32[16,512,128]{2,1,0:T(8,128)S(1)}, f32[16,512,128]{2,1,0:T(8,128)}, u32[]{:S(2)}) copy-start(f32[16,512,128]{2,1,0:T(8,128)} %get-tuple-element.28) | copy-start | bytes 12582916
